TPU v7x, 256 devices: a whole 4x4x8 slice. The times are simulated.
256 devices in a mesh: row: 32 (over x, z), col: 4 (over y_hi, core), ch: 2 (over y_lo).
Axes of the slice: x: 4, y: 4 (y_hi: 2, y_lo: 2; y = y_hi * 2 + y_lo), z: 8, core: 2. Of those that a mesh axis runs over, the one named last changes fastest.
Arguments:
- image_tokens: bfloat16 [512, 1024, 128], P(('row', 'ch'), 'col'), may hold values from -61 to 61
- labels: int32 [512, 1024], P(('row', 'ch'), 'col'), may hold values from 0 to 2
- rel_index: int32 [64, 64], replicated, may hold values from 0 to 224
- norm_gain: float32 [2, 2, 128], replicated, may hold values from 0.25 to 1.75
- norm_shift: float32 [2, 2, 128], replicated, may hold values from -1.5 to 1.5
- qkv_weight: bfloat16 [2, 3, 128, 128], P(None, None, None, 'ch'), may hold values from -5 to 5
- qkv_bias: float32 [2, 3, 128], P(None, None, 'ch'), may hold values from -1.5 to 1.5
- bias_table: float32 [2, 225, 4], P(None, None, 'ch'), may hold values from -4 to 4
- proj_weight: bfloat16 [2, 128, 128], P(None, 'ch'), may hold values from -0.5 to 0.5
- proj_bias: float32 [2, 128], replicated, may hold values from -1.5 to 1.5
- fc1_weight: bfloat16 [2, 128, 512], P(None, None, 'ch'), may hold values from -0.5 to 0.5
- fc1_bias: float32 [2, 512], P(None, 'ch'), may hold values from -2.5 to 2.5
- fc2_weight: bfloat16 [2, 512, 128], P(None, 'ch'), may hold values from -0.25 to 0.25
- fc2_bias: float32 [2, 128], replicated, may hold values from -1.5 to 1.5
Outputs:
- encoded: bfloat16 [512, 1024, 128], P(('row', 'ch'), 'col')
All inputs are finite; a program needn't handle non-finite values.
Results may differ from a plain program's by a relative error of at most 0.014.
Values may be sent and summed in bfloat16 or wider, within the bound.
A program may use at most 128 MiB of HBM per device.

v0:
```python
import functools
import math

import jax
import jax.numpy as jnp
from jax import lax
from jax.experimental import pallas as pl
from jax.experimental.pallas import tpu as pltpu
from jax.sharding import PartitionSpec as P

WIN = 8
SHIFT = 4
HEADS = 4
EPS = 1e-05
C = 128
HEAD = 32
BF = jnp.bfloat16
F32 = jnp.float32
LOG2E = math.log2(math.e)
QSCALE = LOG2E / math.sqrt(HEAD)
ROOT_HALF = math.sqrt(0.5)
EXCLUDED = -1e30
MESH = pl.DeviceIdType.MESH

GROUP = 8
CHUNK = GROUP * WIN


def norm(x, gain, shift):
    center = x - jnp.mean(x, axis=-1, keepdims=True)
    spread = jnp.mean(center * center, axis=-1, keepdims=True)
    return (center * lax.rsqrt(spread + EPS) * gain + shift).astype(BF)


def dot(a, b):
    return jnp.dot(a, b, preferred_element_type=F32)


def side_by_side(a, b):
    return jnp.concatenate([a.astype(F32), b.astype(F32)], axis=1)


def kernel(
    x_ref, lab_ref, rel_ref, gain_ref, shift_ref, qkvw_ref, qkvb_ref, tbl_ref, projw_ref,
    projb_ref, fc1w_ref, fc1b_ref, fc2w_ref, fc2b_ref,
    out_ref,
    y, ids, wqkv, bqkv, wproj, wturned, bias,
    qk_s, qk_r, v_s, v_r, qkvb_r, tbl_r, fc1b_r, fc1w_r, fc2w_r,
    lab_up, lab_side, lab_diag,
    halo_s, halo_r, side_s, side_r, diag_r,
    att_own, att_s, att_r, att_side, att_diag,
    send, recv,
):
    cols = x_ref.shape[1]
    chunks = cols // CHUNK
    wins = cols // WIN
    groups = lax.axis_size("ch")
    bands = lax.axis_size("row") * groups
    tiles = lax.axis_size("col")
    ch = lax.axis_index("ch")
    col = lax.axis_index("col")
    band = lax.axis_index("row") * groups + ch

    def device(band_step, col_step):
        b = lax.rem(band + bands + band_step, bands)
        c = lax.rem(col + tiles + col_step, tiles)
        return {"row": b // groups, "col": c, "ch": lax.rem(b, groups)}

    partner = {"row": lax.axis_index("row"), "col": col, "ch": 1 - ch}
    up, down = device(-1, 0), device(1, 0)
    left, right = device(0, -1), device(0, 1)
    up_left, down_right = device(-1, -1), device(1, 1)

    barrier = pltpu.get_barrier_semaphore()
    peers = (up, down, left, right, up_left, down_right)
    for peer in peers:
        pl.semaphore_signal(barrier, inc=1, device_id=peer, device_id_type=MESH)

    for b in range(2):
        qk_s[b] = side_by_side(qkvw_ref[b, 0], qkvw_ref[b, 1]).astype(BF)
    v_s[...] = side_by_side(qkvw_ref[0, 2], qkvw_ref[1, 2]).astype(BF)

    pl.semaphore_wait(barrier, len(peers))

    def copy(i, src, dst, to):
        return pltpu.make_async_remote_copy(
            src_ref=src, dst_ref=dst, send_sem=send.at[i], recv_sem=recv.at[i],
            device_id=to, device_id_type=MESH,
        )

    def weight_copies(b):
        return [
            copy(4 + 8 * b, projw_ref.at[b], wproj.at[b, pl.ds(64, 64)], partner),
            copy(5 + 8 * b, fc1w_ref.at[b], fc1w_r.at[b], partner),
            copy(6 + 8 * b, fc2w_ref.at[b], fc2w_r.at[b], partner),
        ]

    first = [
        copy(0, qk_s.at[0], qk_r.at[0], partner),
        copy(1, v_s, v_r, partner),
        copy(2, qkvb_ref, qkvb_r, partner),
        copy(3, tbl_ref, tbl_r, partner),
        copy(7, fc1b_ref, fc1b_r, partner),
    ]
    second = [copy(8, qk_s.at[1], qk_r.at[1], partner)]
    weights = [weight_copies(0), weight_copies(1)]
    label_copies = [
        copy(9, lab_ref, lab_up, up),
        copy(10, lab_ref, lab_side, left),
        copy(11, lab_ref, lab_diag, up_left),
    ]
    for c in first + weights[0] + label_copies + second + weights[1]:
        c.start()

    lane = lax.broadcasted_iota(jnp.int32, (1, C), 1)
    head_of = lane // HEAD
    heads = [(head_of == h).astype(F32).astype(BF) for h in range(HEADS)]

    for b in range(2):
        wproj[b, 0:64] = projw_ref[b]

    for c in first:
        c.wait_recv()

    def merge(b):
        wqkv[b, :, 0:128] = side_by_side(qkvw_ref[b, 0], qk_r[b, :, 0:64]).astype(BF)
        wqkv[b, :, 128:256] = side_by_side(qkvw_ref[b, 1], qk_r[b, :, 64:128]).astype(BF)
        wqkv[b, :, 256:384] = side_by_side(
            qkvw_ref[b, 2], v_r[:, 64 * b : 64 * b + 64]
        ).astype(BF)
        bqkv[b, 0:3] = side_by_side(qkvb_ref[b], qkvb_r[b])

    rel = rel_ref[...]
    low = rel < 128
    within = jnp.bitwise_and(rel, 127)
    left_half = lane < 64
    for b in range(2):
        for tile, source in enumerate((tbl_ref, tbl_r)):
            picked = []
            for h in range(2):
                row = 4 * b + 2 * h
                a0 = jnp.broadcast_to(source[row : row + 1], rel.shape)
                a1 = jnp.broadcast_to(source[row + 1 : row + 2], rel.shape)
                g0 = jnp.take_along_axis(a0, within, axis=1)
                g1 = jnp.take_along_axis(a1, within, axis=1)
                picked.append(jnp.where(low, g0, g1))
            bias[b, :, 128 * tile : 128 * tile + 128] = (
                jnp.where(left_half, picked[0], picked[1]) * LOG2E
            )

    def qkv(b, tokens):
        n = norm(tokens, gain_ref[b, 0:1], shift_ref[b, 0:1])
        r = dot(n, wqkv[b])
        q = ((r[:, 0:128] + bqkv[b, 0:1]) * QSCALE).astype(BF)
        k = (r[:, 128:256] + bqkv[b, 1:2]).astype(BF)
        v = (r[:, 256:384] + bqkv[b, 2:3]).astype(BF)
        return q, k, v

    def attend(b, q, k, v, allowed):
        stacked = jnp.concatenate([q * m for m in heads], axis=0)
        s = lax.dot_general(
            k, stacked, (((1,), (1,)), ((), ())), preferred_element_type=F32
        )
        s = s + bias[b]
        if allowed is not None:
            s = jnp.concatenate(
                [jnp.where(allowed, s[:, 0:128], EXCLUDED),
                 jnp.where(allowed, s[:, 128:256], EXCLUDED)], axis=1)
        raised = jnp.exp2(s - jnp.max(s, axis=0, keepdims=True))
        w = (raised * (1.0 / jnp.sum(raised, axis=0, keepdims=True))).astype(BF)
        o = lax.dot_general(w, v, (((0,), (0,)), ((), ())), preferred_element_type=F32)
        mixed = o[192:256]
        for h in (2, 1, 0):
            mixed = jnp.where(head_of == h, o[64 * h : 64 * h + 64], mixed)
        return mixed.astype(BF)

    def feed(b, attended, tokens, proj):
        mid = (tokens + dot(attended, proj) + projb_ref[b : b + 1]).astype(BF).astype(F32)
        n = norm(mid, gain_ref[b, 1:2], shift_ref[b, 1:2])
        total = mid + fc2b_ref[b : b + 1]
        for w1, b1, w2 in (
            (fc1w_ref, fc1b_ref, fc2w_ref), (fc1w_r, fc1b_r, fc2w_r)
        ):
            inner = dot(n, w1[b]) + b1[b : b + 1]
            hidden = (inner * (0.5 + 0.5 * lax.erf(inner * ROOT_HALF))).astype(BF)
            total = total + dot(hidden, w2[b])
        return total.astype(BF).astype(F32)

    def slab(r, at):
        return y[r, pl.ds(at, WIN), :]

    merge(0)
    for c in weights[0]:
        c.wait_recv()

    def halo_copy(j):
        at = pl.ds(pl.multiple_of(j * CHUNK, CHUNK), CHUNK)
        return copy(20 + j, halo_s.at[:, at], halo_r.at[:, at], up)

    def first_block(j, carry):
        base = pl.multiple_of(j * CHUNK, CHUNK)
        rows = [x_ref[r, pl.ds(base, CHUNK), :].astype(F32) for r in range(WIN)]
        tokens = jnp.concatenate(
            [rows[r][WIN * g : WIN * g + WIN] for g in range(GROUP) for r in range(WIN)], axis=0
        )
        q, k, v = qkv(0, tokens)
        attended = jnp.concatenate(
            [attend(0, *(a[64 * g : 64 * g + 64] for a in (q, k, v)), None) for g in range(GROUP)],
            axis=0,
        )
        done = feed(0, attended, tokens, wproj[0])
        for r in range(WIN):
            line = jnp.concatenate(
                [done[64 * g + 8 * r : 64 * g + 8 * r + 8] for g in range(GROUP)], axis=0
            )
            y[r, pl.ds(base, CHUNK), :] = line
            if r < SHIFT:
                halo_s[r, pl.ds(base, CHUNK), :] = line.astype(BF)
        halo_copy(j).start()
        return carry

    lax.fori_loop(0, chunks, first_block, 0)

    for r in range(SHIFT):
        side_s[r] = y[SHIFT + r, 0:16, :].astype(BF)
    patches = [
        copy(12 + 28, side_s, side_r, left),
        copy(13 + 28, halo_s.at[:, pl.ds(0, 16)], diag_r, up_left),
    ]
    for c in patches:
        c.start()

    for c in label_copies:
        c.wait_recv()
    last_band = (band == bands - 1).astype(jnp.int32) * 2
    last_tile = (col == tiles - 1).astype(jnp.int32)
    for r in range(WIN):
        if r < SHIFT:
            own, beside, extra = lab_ref, lab_side, 0
            at = SHIFT + r
        else:
            own, beside, extra = lab_up, lab_diag, last_band
            at = r - SHIFT
        for t in range(cols // 128):
            line = own[at : at + 1, 128 * t : 128 * t + 128] * 4 + extra
            ids[r, 128 * t : 128 * t + 128, :] = jnp.broadcast_to(line.astype(F32), (128, 128)).T
        line = beside[at : at + 1, 0:128] * 4 + extra + last_tile
        ids[r, cols : cols + 8, :] = jnp.broadcast_to(line.astype(F32), (128, 128)).T[0:8]

    for c in second:
        c.wait_recv()
    merge(1)

    for j in range(chunks):
        halo_copy(j).wait_recv()
    for c in patches:
        c.wait_recv()
    for r in range(SHIFT):
        y[WIN + r, 0:cols, :] = halo_r[r].astype(F32)
        y[SHIFT + r, cols : cols + 8, :] = side_r[r].astype(F32)[0:8]
        y[WIN + r, cols : cols + 8, :] = diag_r[r].astype(F32)[0:8]

    def attended_copy(j):
        at = pl.ds(pl.multiple_of(j * 32 * GROUP, 32 * GROUP), 32 * GROUP)
        return copy(28 + j, att_s.at[at], att_r.at[at], down)

    def second_attention(j, carry):
        base = pl.multiple_of(j * CHUNK, CHUNK)
        tokens = jnp.concatenate(
            [slab(SHIFT + r, base + SHIFT + WIN * g) for g in range(GROUP) for r in range(WIN)],
            axis=0,
        )
        q, k, v = qkv(1, tokens)
        for g in range(GROUP):
            mine = jnp.concatenate(
                [ids[r, pl.ds(base + SHIFT + WIN * g, WIN), :] for r in range(WIN)], axis=0
            )
            other = jnp.concatenate([mine, mine], axis=0).T[0:64]
            o = attend(1, *(a[64 * g : 64 * g + 64] for a in (q, k, v)), mine == other)
            at = pl.ds(pl.multiple_of(j * 32 * GROUP, 32 * GROUP) + 32 * g, 32)
            att_own[at, :] = o[0:32]
            att_s[at, :] = o[32:64]
        attended_copy(j).start()
        return carry

    lax.fori_loop(0, chunks, second_attention, 0)

    final = pl.ds(32 * (wins - 1), 32)
    corner_copies = [
        copy(42, att_own.at[final], att_side, right),
        copy(43, att_s.at[final], att_diag, down_right),
    ]
    for c in corner_copies:
        c.start()
    for r in range(WIN):
        y[r, cols : cols + 8, :] = y[r, 0:8, :]
    for c in weights[1]:
        c.wait_recv()
    wturned[0:64] = wproj[1, 64:128]
    wturned[64:128] = wproj[1, 0:64]

    def second_feed(attended_ref, first_row, proj):
        def body(j, carry):
            base = pl.multiple_of(j * CHUNK, CHUNK)
            at = pl.ds(pl.multiple_of(j * 32 * GROUP, 32 * GROUP), 32 * GROUP)
            where = [
                (first_row + r, base + SHIFT + WIN * g) for g in range(GROUP) for r in range(SHIFT)
            ]
            tokens = jnp.concatenate([slab(*w) for w in where], axis=0)
            done = feed(1, attended_ref[at, :], tokens, proj[...])
            for i, (r, c) in enumerate(where):
                y[r, pl.ds(c, WIN), :] = done[8 * i : 8 * i + 8]
            return carry

        lax.fori_loop(0, chunks, body, 0)

    right_part = jnp.bitwise_and(lax.broadcasted_iota(jnp.int32, (32, C), 0), 7) >= SHIFT
    def put_corner(target, source):
        target[final, :] = jnp.where(
            right_part, source[...].astype(F32), target[final, :].astype(F32)
        ).astype(BF)

    corner_copies[0].wait()
    put_corner(att_own, att_side)
    second_feed(att_own, SHIFT, wproj.at[1])
    for j in range(chunks):
        attended_copy(j).wait_recv()
    corner_copies[1].wait()
    put_corner(att_r, att_diag)
    second_feed(att_r, 0, wturned)

    for r in range(WIN):
        head_cols = y[r, cols : cols + 8, :]
        keep = lax.broadcasted_iota(jnp.int32, (8, C), 0) < SHIFT
        y[r, 0:8, :] = jnp.where(keep, head_cols, y[r, 0:8, :])
        out_ref[r] = y[r, 0:cols, :].astype(BF)

    for c in first + second + weights[0] + weights[1] + label_copies + patches:
        c.wait_send()
    for j in range(chunks):
        halo_copy(j).wait_send()
        attended_copy(j).wait_send()


def on_device(
    image_tokens, labels, rel_index, norm_gain, norm_shift, qkv_weight, qkv_bias, bias_table,
    proj_weight, proj_bias, fc1_weight, fc1_bias, fc2_weight, fc2_bias,
):
    rows, cols, _ = image_tokens.shape
    wins = cols // WIN
    rel = jnp.tile(rel_index.T, (1, 2))
    entries = bias_table.shape[1]
    table = jnp.pad(
        jnp.transpose(bias_table, (0, 2, 1)), ((0, 0), (0, 0), (0, 256 - entries))
    ).reshape(8, 128)
    vmem = pl.BlockSpec(memory_space=pltpu.VMEM)
    args = (
        image_tokens, labels, rel, norm_gain, norm_shift, qkv_weight, qkv_bias, table,
        proj_weight, proj_bias, fc1_weight, fc1_bias, fc2_weight, fc2_bias,
    )
    V = pltpu.VMEM
    copies = 44
    return pl.pallas_call(
        kernel,
        out_shape=jax.ShapeDtypeStruct((rows, cols, C), BF),
        in_specs=[vmem] * len(args),
        out_specs=vmem,
        scratch_shapes=[
            V((rows + SHIFT, cols + 8, C), F32),
            V((rows, cols + 8, C), F32),
            V((2, C, 3 * C), BF),
            V((2, 3, C), F32),
            V((2, C, C), BF),
            V((C, C), BF),
            V((2, 64, 256), F32),
            V((2, C, C), BF), V((2, C, C), BF),
            V((C, C), BF), V((C, C), BF),
            V(qkv_bias.shape, F32), V((8, 128), F32), V(fc1_bias.shape, F32),
            V(fc1_weight.shape, BF), V(fc2_weight.shape, BF),
            V(labels.shape, jnp.int32), V(labels.shape, jnp.int32), V(labels.shape, jnp.int32),
            V((SHIFT, cols, C), BF), V((SHIFT, cols, C), BF),
            V((SHIFT, 16, C), BF), V((SHIFT, 16, C), BF), V((SHIFT, 16, C), BF),
            V((32 * wins, C), BF), V((32 * wins, C), BF), V((32 * wins, C), BF),
            V((32, C), BF), V((32, C), BF),
            pltpu.SemaphoreType.DMA((copies,)),
            pltpu.SemaphoreType.DMA((copies,)),
        ],
        compiler_params=pltpu.CompilerParams(
            collective_id=0, has_side_effects=True, vmem_limit_bytes=60 * 1024 * 1024
        ),
        name="swin_pair",
    )(*args)


def solution(mesh):
    in_specs = (
        P(("row", "ch"), "col", None),
        P(("row", "ch"), "col"),
        P(),
        P(),
        P(),
        P(None, None, None, "ch"),
        P(None, None, "ch"),
        P(None, None, "ch"),
        P(None, "ch", None),
        P(),
        P(None, None, "ch"),
        P(None, "ch"),
        P(None, "ch", None),
        P(),
    )
    out_specs = P(("row", "ch"), "col", None)
    return jax.shard_map(
        on_device, mesh=mesh, in_specs=in_specs, out_specs=out_specs, check_vma=False
    )
```

profile of v0, /device:TPU:1, one launch (start us, length us, event | category | flops | bytes accessed | tf_op | source)
XLA Modules:
  0.0 60.4 jit_solution(2129037016384366632)
XLA Ops:
  0.0 0.0 copy-start.2
  0.0 0.0 copy-start.1
  0.0 0.7 %copy-done.2 = f32[2,3,64]{2,0,1:T(2,128)S(1)} copy-done((f32[2,3,64]{2,0,1:T(2,128)S(1)}, f32[2,3,64]{2,0,1:T(2,128)}, u32[]{:S(2)}) %copy-start.2) | copy-done | bytes 1560
  0.7 0.6 copy.17.qkvb_ref
  1.3 0.0 copy-done.1
  1.3 0.6 reshape.7.tbl_ref
  1.9 0.8 %copy.15 = s32[64,64]{1,0:T(8,128)S(1)} copy(s32[64,64]{0,1:T(8,128)} %bitcast.2) | data formatting | bytes 32768 | tf_op jit(solution)/shard_map/transpose | solution.py:351
  2.7 0.0 copy-start
  2.7 0.7 %tile.10.rel_ref = s32[64,128]{1,0:T(8,128)} reshape(s32[64,2,64]{2,1,0:T(2,128)S(1)} %tile.4) | data formatting | bytes 65536 | tf_op jit(solution)/shard_map/tile | solution.py:351
  3.5 0.1 copy-done
  3.6 0.8 %copy.16.qkvw_ref = bf16[2,3,128,64]{3,2,1,0:T(8,128)(2,1)} copy(bf16[2,3,128,64]{2,3,1,0:T(8,128)(2,1)S(1)} %copy-done) | data formatting | bytes 196608 | tf_op args[5]
  4.4 54.1 %swin_pair.1 = bf16[8,256,128]{2,1,0:T(8,128)(2,1)} custom-call(bf16[8,256,128]{2,1,0:T(8,128)(2,1)} %x_ref.1, s32[8,256]{1,0:T(8,128)} %lab_ref.1, s32[64,128]{1,0:T(8,128)} %tile.10.rel_ref, f32[2,2,128]{2,1,0:T(2,128)} %gain_ref.1, f32[2,2,128]{2,1,0:T(2,128)} %shift_ref.1, bf16[2,3,128,64]{3,2,1,0:T(8,128)(2,1)} %copy.16.qkvw_ref, ...), custom_call_target="tpu_custom_call" | custom-call | tf_op jit(solution)/shard_map/swin_pair/pallas_call | solution.py:363
  58.6 1.9 %copy.19 = bf16[8,256,128]{2,1,0:T(8,128)(2,1)} copy(bf16[8,256,128]{2,1,0:T(8,128)(2,1)} %swin_pair.1) | data formatting | bytes 1048576
  (2 shorter events, 0.0 us)
Async XLA Ops:
  0.0 0.7 %copy-start.2 = (f32[2,3,64]{2,0,1:T(2,128)S(1)}, f32[2,3,64]{2,0,1:T(2,128)}, u32[]{:S(2)}) copy-start(f32[2,3,64]{2,0,1:T(2,128)} %param.20) | copy-start | bytes 4612
  0.0 1.3 %copy-start.1 = (f32[2,225,2]{1,2,0:T(2,128)S(1)}, f32[2,225,2]{1,2,0:T(2,128)}, u32[]{:S(2)}) copy-start(f32[2,225,2]{1,2,0:T(2,128)} %param.21) | copy-start | bytes 10804
  2.7 0.9 %copy-start = (bf16[2,3,128,64]{2,3,1,0:T(8,128)(2,1)S(1)}, bf16[2,3,128,64]{2,3,1,0:T(8,128)(2,1)}, u32[]{:S(2)}) copy-start(bf16[2,3,128,64]{2,3,1,0:T(8,128)(2,1)} %param.19) | copy-start | bytes 294916
where the time goes:
time: 61.4 us; the launch traced here: 60.4 us
  Pallas kernels  54.1 us (88%)
  local copies, waits for them, and re-layouts  6.28 us (10%)
    pallas_call x1, Pallas kernels, on_device(): pl.pallas_call(kernel, out_shape=jax.ShapeDtypeStruct((rows, cols, C), BF...  54.1 us
    unnamed x9, local copies, waits for them, and re-layouts  4.12 us

commit v1 on v0

v1 whole, which is shorter than its diff:
```python
import functools
import math

import jax
import jax.numpy as jnp
from jax import lax
from jax.experimental import pallas as pl
from jax.experimental.pallas import tpu as pltpu
from jax.sharding import PartitionSpec as P

WIN = 8
SHIFT = 4
HEADS = 4
EPS = 1e-05
C = 128
HEAD = 32
BF = jnp.bfloat16
F32 = jnp.float32
LOG2E = math.log2(math.e)
QSCALE = LOG2E / math.sqrt(HEAD)
ROOT_HALF = math.sqrt(0.5)
EXCLUDED = -1e30
MESH = pl.DeviceIdType.MESH

GROUP = 8
CHUNK = GROUP * WIN
SPANS = 3


def norm(x, gain, shift):
    center = x - jnp.mean(x, axis=-1, keepdims=True)
    spread = jnp.mean(center * center, axis=-1, keepdims=True)
    return (center * lax.rsqrt(spread + EPS) * gain + shift).astype(BF)


def dot(a, b):
    return jnp.dot(a, b, preferred_element_type=F32)


def dot_rows(a, b):
    return lax.dot_general(a, b, (((1,), (1,)), ((), ())), preferred_element_type=F32)


def dot_first(a, b):
    return lax.dot_general(a, b, (((0,), (0,)), ((), ())), preferred_element_type=F32)


def kernel(
    x_in, lab_in, rel_in, gain_in, shift_in, qkvw_in, qkvb_in, tbl_in, projw_in,
    projb_in, fc1w_in, fc1b_in, fc2w_in, fc2b_in,
    out_ref,
    x, lab, rel, gain, shift, qkvb, tbl, wproj, projb, w1, b1, w2, fc2b,
    wown, woth, wfull, bqkv, bias0, bias1,
    y, ids, normed, att, result, region, labs,
    halo, both, sides, corners,
    local, send, recv,
):
    cols = x.shape[1]
    chunks = cols // CHUNK
    wins = cols // WIN + 1
    span = wins // SPANS
    groups = lax.axis_size("ch")
    bands = lax.axis_size("row") * groups
    tiles = lax.axis_size("col")
    ch = lax.axis_index("ch")
    col = lax.axis_index("col")
    band = lax.axis_index("row") * groups + ch

    def device(band_step, col_step):
        b = lax.rem(band + bands + band_step, bands)
        c = lax.rem(col + tiles + col_step, tiles)
        return {"row": b // groups, "col": c, "ch": lax.rem(b, groups)}

    partner = {"row": lax.axis_index("row"), "col": col, "ch": 1 - ch}
    up, down = device(-1, 0), device(1, 0)
    left, right = device(0, -1), device(0, 1)
    diagonals = [device(i, j) for i in (-1, 1) for j in (-1, 1)]

    barrier = pltpu.get_barrier_semaphore()
    peers = [up, down, left, right] + diagonals
    for peer in peers:
        pl.semaphore_signal(barrier, inc=1, device_id=peer, device_id_type=MESH)

    def load(i, src, dst):
        return pltpu.make_async_copy(src, dst, local.at[i])

    own_rows = pl.ds(0, 64)
    other_rows = pl.ds(64, 64)
    early = [
        load(0, x_in, x),
        load(1, qkvw_in.at[0], wown.at[:, own_rows]),
        load(2, qkvb_in, qkvb.at[0]),
        load(3, tbl_in, tbl.at[0]),
        load(4, rel_in, rel),
        load(5, gain_in, gain),
        load(6, shift_in, shift),
    ]
    late = [
        load(7, projw_in, wproj.at[:, own_rows]),
        load(8, fc1w_in, w1.at[0]),
        load(9, fc1b_in, b1.at[0]),
        load(10, fc2w_in, w2.at[0]),
        load(11, qkvw_in.at[1], wfull.at[:, own_rows]),
        load(12, projb_in, projb),
        load(13, fc2b_in, fc2b),
        load(14, lab_in, lab),
    ]
    for c in early + late:
        c.start()

    wown[:, 64:128, :] = jnp.zeros((3, 64, C), BF)
    woth[:, 0:64, :] = jnp.zeros((3, 64, C), BF)

    def copy(i, src, dst, to):
        return pltpu.make_async_remote_copy(
            src_ref=src, dst_ref=dst, send_sem=send.at[i], recv_sem=recv.at[i],
            device_id=to, device_id_type=MESH,
        )

    first = [
        copy(0, wown.at[:, own_rows], woth.at[:, other_rows], partner),
        copy(1, qkvb.at[0], qkvb.at[1], partner),
        copy(2, tbl.at[0], tbl.at[1], partner),
        copy(3, b1.at[0], b1.at[1], partner),
    ]
    def feed_copies(b):
        return [
            copy(4 + 4 * b, wproj.at[b, own_rows], wproj.at[b, other_rows], partner),
            copy(5 + 4 * b, w1.at[0, b], w1.at[1, b], partner),
            copy(6 + 4 * b, w2.at[0, b], w2.at[1, b], partner),
        ]
    second = feed_copies(0)
    third = [copy(7, wfull.at[:, own_rows], wfull.at[:, other_rows], partner)] + feed_copies(1)
    half_at = {-1: pl.ds(0, 128), 1: pl.ds(cols - 128, 128)}
    region_copies = [copy(11, region, labs.at[0], up), copy(12, region, labs.at[1], down)] + [
        copy(13 + i, region.at[:, half_at[side]], labs.at[2 + i, :, pl.ds(0, 128)], to)
        for i, (side, to) in enumerate(
            [(-1, left), (1, right)] + list(zip((-1, 1, -1, 1), diagonals))
        )
    ]

    for c in early:
        c.wait()

    lane = lax.broadcasted_iota(jnp.int32, (1, C), 1)
    head_of = lane // HEAD
    heads = [(head_of == h).astype(F32).astype(BF) for h in range(HEADS)]

    entries = tbl.shape[-1]
    relt = rel[...].astype(F32).T

    def lookup(index, side, b, h):
        index = index.astype(jnp.int32)
        line = tbl[side, b, h : h + 1, :]
        a0 = jnp.broadcast_to(line[:, 0:128], index.shape)
        a1 = jnp.concatenate([line[:, 128:], jnp.zeros((1, 256 - entries), F32)], axis=1)
        a1 = jnp.broadcast_to(a1, index.shape)
        within = jnp.bitwise_and(index, 127)
        g0 = jnp.take_along_axis(a0, within, axis=1)
        g1 = jnp.take_along_axis(a1, within, axis=1)
        return jnp.where(index < 128, g0, g1) * LOG2E

    twice = jnp.concatenate([relt, relt], axis=1)

    def first_bias(side):
        bias0[:, 128 * side : 128 * side + 128] = jnp.where(
            lane < 64, lookup(twice, side, 0, 0), lookup(twice, side, 0, 1)
        )

    def zero_padded(values, side):
        pad = jnp.zeros_like(values)
        return jnp.concatenate([values, pad] if side == 0 else [pad, values], axis=1)

    first_bias(0)
    for m in range(3):
        bqkv[0, m : m + 1] = zero_padded(qkvb[0, m, 0:1], 0)

    def project(n, w, b):
        r = dot_rows(n, w[...].reshape(3 * C, C))
        q = ((r[:, 0:128] + bqkv[b, 0:1]) * QSCALE).astype(BF)
        k = (r[:, 128:256] + bqkv[b, 1:2]).astype(BF)
        v = (r[:, 256:384] + bqkv[b, 2:3]).astype(BF)
        return q, k, v

    def softmax(s):
        raised = jnp.exp2(s - jnp.max(s, axis=0, keepdims=True))
        return (raised * (1.0 / jnp.sum(raised, axis=0, keepdims=True))).astype(BF)

    def half_attention(side, q, k, v):
        stacked = jnp.concatenate([q * heads[2 * side], q * heads[2 * side + 1]], axis=0)
        s = dot_rows(k, stacked) + bias0[:, 128 * side : 128 * side + 128]
        o = dot_first(softmax(s), v)
        return jnp.where(head_of == 2 * side, o[0:64], o[64:128]).astype(BF)

    def windows_of(base):
        lines = [x[r, pl.ds(base, CHUNK), :].astype(F32) for r in range(WIN)]
        return jnp.concatenate(
            [lines[r][WIN * g : WIN * g + WIN] for g in range(GROUP) for r in range(WIN)], axis=0
        )

    def own_heads(j, carry):
        base = pl.multiple_of(j * CHUNK, CHUNK)
        at = pl.ds(pl.multiple_of(j * 64 * GROUP, 64 * GROUP), 64 * GROUP)
        n = norm(windows_of(base), gain[0, 0:1], shift[0, 0:1])
        normed[at, :] = n
        q, k, v = project(n, wown, 0)
        att[at, :] = jnp.concatenate(
            [half_attention(0, *(a[64 * g : 64 * g + 64] for a in (q, k, v))) for g in range(GROUP)],
            axis=0,
        )
        return carry

    lax.fori_loop(0, chunks, own_heads, 0)

    for c in late:
        c.wait()
    i = lax.broadcasted_iota(jnp.int32, lab.shape, 0)
    j = lax.broadcasted_iota(jnp.int32, lab.shape, 1)
    first_band = (band == 0).astype(jnp.int32)
    first_tile = (col == 0).astype(jnp.int32)
    region[...] = (
        lab[...] * 4
        + (i < SHIFT).astype(jnp.int32) * (2 * first_band)
        + (j < SHIFT).astype(jnp.int32) * first_tile
    )

    pl.semaphore_wait(barrier, len(peers))
    for c in first + second + region_copies + third:
        c.start()

    for c in first:
        c.wait_recv()
    first_bias(1)
    for m in range(3):
        bqkv[1, m : m + 1] = zero_padded(qkvb[1, m, 0:1], 1)
        bqkv[2, m : m + 1] = jnp.concatenate([qkvb[0, m, 1:2], qkvb[1, m, 1:2]], axis=1)
    for t, turned in enumerate(
        (relt[:, 0:32], jnp.concatenate([relt[32:64, 32:64], relt[0:32, 32:64]], axis=0))
    ):
        index = jnp.concatenate([turned] * 4, axis=1)
        picked = lookup(index, 1, 1, 1)
        for h in (2, 1, 0):
            picked = jnp.where(head_of == h, lookup(index, h // 2, 1, h % 2), picked)
        bias1[t] = picked

    def feed(b, attended, tokens):
        mid = (tokens + dot(attended, wproj[b]) + projb[b : b + 1]).astype(BF).astype(F32)
        n = norm(mid, gain[b, 1:2], shift[b, 1:2])
        total = mid + fc2b[b : b + 1]
        for side in range(2):
            inner = dot(n, w1[side, b]) + b1[side, b : b + 1]
            hidden = (inner * (0.5 + 0.5 * lax.erf(inner * ROOT_HALF))).astype(BF)
            total = total + dot(hidden, w2[side, b])
        return total.astype(BF).astype(F32)

    for c in second:
        c.wait_recv()

    def halo_copies(k):
        at = pl.ds(pl.multiple_of(k * CHUNK, CHUNK), CHUNK)
        return (
            copy(20 + k, halo.at[pl.ds(0, SHIFT), at], both.at[0, :, at], up),
            copy(24 + k, halo.at[pl.ds(SHIFT, SHIFT), at], both.at[1, :, at], down),
        )

    def first_block(k, carry):
        base = pl.multiple_of(k * CHUNK, CHUNK)
        at = pl.ds(pl.multiple_of(k * 64 * GROUP, 64 * GROUP), 64 * GROUP)
        q, key, v = project(normed[at, :], woth, 1)
        other = jnp.concatenate(
            [half_attention(1, *(a[64 * g : 64 * g + 64] for a in (q, key, v))) for g in range(GROUP)],
            axis=0,
        )
        done = feed(0, att[at, :] + other, windows_of(base))
        for r in range(WIN):
            line = jnp.concatenate(
                [done[64 * g + 8 * r : 64 * g + 8 * r + 8] for g in range(GROUP)], axis=0
            )
            y[SHIFT + r, pl.ds(base + SHIFT, CHUNK), :] = line
            halo[r, pl.ds(base, CHUNK), :] = line.astype(BF)
        for c in halo_copies(k):
            c.start()
        return carry

    lax.fori_loop(0, chunks, first_block, 0)

    edge = {-1: pl.ds(0, 16), 1: pl.ds(cols - 16, 16)}
    edge_copies = [
        copy(28, halo.at[:, edge[-1]], sides.at[1], left),
        copy(29, halo.at[:, edge[1]], sides.at[0], right),
    ] + [
        copy(30 + i, halo.at[pl.ds(r0, SHIFT), edge[side]], corners.at[i], to)
        for i, ((r0, side), to) in enumerate(
            zip(((0, -1), (0, 1), (SHIFT, -1), (SHIFT, 1)), diagonals)
        )
    ]
    for c in edge_copies:
        c.start()

    for c in region_copies:
        c.wait_recv()

    def spread(line):
        return jnp.broadcast_to(line.astype(F32), (128, 128)).T

    for r in range(2 * WIN):
        if r < SHIFT:
            middle, before, after, at = labs.at[1], labs.at[7], labs.at[6], SHIFT + r
        elif r < SHIFT + WIN:
            middle, before, after, at = region, labs.at[3], labs.at[2], r - SHIFT
        else:
            middle, before, after, at = labs.at[0], labs.at[5], labs.at[4], r - SHIFT - WIN
        for t in range(cols // 128):
            ids[r, SHIFT + 128 * t : SHIFT + 128 * t + 128, :] = spread(
                middle[at : at + 1, 128 * t : 128 * t + 128]
            )
        ids[r, 0:SHIFT, :] = spread(before[at : at + 1, 0:128])[128 - SHIFT :]
        ids[r, SHIFT + cols : 2 * SHIFT + cols, :] = spread(after[at : at + 1, 0:128])[0:SHIFT]

    for c in third:
        c.wait_recv()
    for c in edge_copies[0:2]:
        c.wait_recv()
    ends = ((slice(0, SHIFT), slice(12, 16)), (slice(SHIFT + cols, 2 * SHIFT + cols), slice(0, SHIFT)))
    for s, (to, of) in enumerate(ends):
        for r in range(WIN):
            y[SHIFT + r, to, :] = sides[s, r].astype(F32)[of]

    def shifted_band(is_bottom):
        mine = SHIFT + SHIFT * is_bottom
        theirs = (SHIFT + WIN) * is_bottom

        arrived = both.at[1 - is_bottom]
        flow = 20 + 4 * (1 - is_bottom)

        def take(k):
            at = pl.ds(pl.multiple_of(k * CHUNK, CHUNK), CHUNK)
            copy(flow + k, arrived.at[:, at], arrived.at[:, at], up).wait_recv()
            for r in range(SHIFT):
                y[theirs + r, pl.ds(k * CHUNK + SHIFT, CHUNK), :] = arrived[r, at, :].astype(F32)

        corner = 2 * (1 - is_bottom)
        for i in range(2):
            part = corners.at[corner + i]
            copy(30 + corner + i, part, part, up).wait_recv()
            to, of = ends[1 - i]
            for r in range(SHIFT):
                y[theirs + r, to, :] = part[r].astype(F32)[of]
        take(0)

        def body(c, carry):
            take(c + 1)
            base = pl.multiple_of(c * span * WIN, WIN)

            def gather(ref, row):
                return [
                    [ref[row + r, pl.ds(base + WIN * g, WIN), :] for r in range(SHIFT)]
                    for g in range(span)
                ]

            own = gather(y, mine)
            beside = gather(y, theirs)
            own_id = gather(ids, mine)
            beside_id = gather(ids, theirs)
            flat = lambda parts: jnp.concatenate([p for g in parts for p in g], axis=0)
            tokens = flat(own)
            n = norm(tokens, gain[1, 0:1], shift[1, 0:1])
            n2 = norm(flat(beside), gain[1, 0:1], shift[1, 0:1])
            q, k, v = project(n, wfull, 2)
            r2 = dot_rows(n2, wfull[1:3].reshape(2 * C, C))
            k2 = (r2[:, 0:128] + bqkv[2, 1:2]).astype(BF)
            v2 = (r2[:, 128:256] + bqkv[2, 2:3]).astype(BF)
            attended = []
            for g in range(span):
                at = slice(32 * g, 32 * g + 32)
                keys = jnp.concatenate([k[at], k2[at]], axis=0)
                values = jnp.concatenate([v[at], v2[at]], axis=0)
                stacked = jnp.concatenate([q[at] * m for m in heads], axis=0)
                s = dot_rows(keys, stacked) + bias1[1 - is_bottom]
                key_id = jnp.concatenate(own_id[g] + beside_id[g], axis=0)
                query_id = jnp.concatenate(own_id[g] * 4, axis=0).T[0:8]
                allowed = key_id == jnp.concatenate([query_id] * 8, axis=0)
                o = dot_first(softmax(jnp.where(allowed, s, EXCLUDED)), values)
                mixed = o[96:128]
                for h in (2, 1, 0):
                    mixed = jnp.where(head_of == h, o[32 * h : 32 * h + 32], mixed)
                attended.append(mixed.astype(BF))
            done = feed(1, jnp.concatenate(attended, axis=0), tokens)
            for g in range(span):
                for r in range(SHIFT):
                    i = 32 * g + 8 * r
                    y[mine + r, pl.ds(base + WIN * g, WIN), :] = done[i : i + 8]
            return carry

        lax.fori_loop(0, SPANS, body, 0)
        row = SHIFT * is_bottom
        for r in range(SHIFT):
            result[row + r] = y[mine + r, SHIFT : SHIFT + cols, :].astype(BF)
        return pltpu.make_async_copy(
            result.at[pl.ds(row, SHIFT)], out_ref.at[pl.ds(row, SHIFT)], local.at[15 + is_bottom]
        )

    near = 1 - ch
    outs = []
    for is_bottom in (near, 1 - near):
        c = shifted_band(is_bottom)
        c.start()
        outs.append(c)
    for c in outs:
        c.wait()

    for c in first + second + third + region_copies + edge_copies:
        c.wait_send()
    for k in range(chunks):
        for c in halo_copies(k):
            c.wait_send()


def on_device(
    image_tokens, labels, rel_index, norm_gain, norm_shift, qkv_weight, qkv_bias, bias_table,
    proj_weight, proj_bias, fc1_weight, fc1_bias, fc2_weight, fc2_bias,
):
    rows, cols, _ = image_tokens.shape
    args = (
        image_tokens, labels, rel_index, norm_gain, norm_shift,
        jnp.swapaxes(qkv_weight, 2, 3), jnp.swapaxes(qkv_bias, 0, 1),
        jnp.swapaxes(bias_table, 1, 2),
        proj_weight, proj_bias, fc1_weight, fc1_bias, fc2_weight, fc2_bias,
    )
    V = pltpu.VMEM
    like = lambda a, *lead: V((*lead, *a.shape), a.dtype)
    copies = 34
    return pl.pallas_call(
        kernel,
        out_shape=jax.ShapeDtypeStruct((rows, cols, C), BF),
        in_specs=[pl.BlockSpec(memory_space=pl.ANY)] * len(args),
        out_specs=pl.BlockSpec(memory_space=pl.ANY),
        scratch_shapes=[
            like(image_tokens), like(labels), like(rel_index), like(norm_gain), like(norm_shift),
            like(args[6], 2), like(args[7], 2),
            V((2, C, C), BF), like(proj_bias),
            like(fc1_weight, 2), like(fc1_bias, 2), like(fc2_weight, 2), like(fc2_bias),
            V((3, C, C), BF), V((3, C, C), BF), V((3, C, C), BF),
            V((3, 3, C), F32),
            V((64, 256), F32), V((2, 64, C), F32),
            V((2 * WIN, cols + 8, C), F32), V((2 * WIN, cols + 8, C), F32),
            V((rows * cols, C), BF), V((rows * cols, C), BF),
            V((rows, cols, C), BF),
            like(labels), like(labels, 8),
            V((rows, cols, C), BF), V((2, SHIFT, cols, C), BF),
            V((2, rows, 16, C), BF), V((4, SHIFT, 16, C), BF),
            pltpu.SemaphoreType.DMA((17,)),
            pltpu.SemaphoreType.DMA((copies,)),
            pltpu.SemaphoreType.DMA((copies,)),
        ],
        compiler_params=pltpu.CompilerParams(
            collective_id=0, has_side_effects=True, vmem_limit_bytes=60 * 1024 * 1024
        ),
        name="swin_pair",
    )(*args)


def solution(mesh):
    in_specs = (
        P(("row", "ch"), "col", None),
        P(("row", "ch"), "col"),
        P(),
        P(),
        P(),
        P(None, None, None, "ch"),
        P(None, None, "ch"),
        P(None, None, "ch"),
        P(None, "ch", None),
        P(),
        P(None, None, "ch"),
        P(None, "ch"),
        P(None, "ch", None),
        P(),
    )
    out_specs = P(("row", "ch"), "col", None)
    return jax.shard_map(
        on_device, mesh=mesh, in_specs=in_specs, out_specs=out_specs, check_vma=False
    )
```

time: 61.4 us -> 64.4 us (1.049); the launches traced: 60.4 us -> 64.2 us
  Pallas kernels: 54.1 us -> 62.4 us
  local copies, waits for them, and re-layouts: 6.28 us -> 1.87 us
    pallas_call x1, Pallas kernels: 54.1 us -> 62.4 us  [on_device(): pl.pallas_call(kernel, out_shape=jax.ShapeDtypeStruct((rows, cols, C), BF...]
    unnamed x9 -> x1, local copies, waits for them, and re-layouts: 4.12 us -> 1.87 us
    transpose x1 -> x0, local copies, waits for them, and re-layouts: 0.83 us -> none  [on_device(): rel = jnp.tile(rel_index.T, (1, 2))]
    another operation x2 -> x0, local copies, waits for them, and re-layouts: 0.74 us -> none  [on_device(): rel = jnp.tile(rel_index.T, (1, 2))]
where the time goes in v1:
time: 64.4 us; the launch traced here: 64.2 us
  Pallas kernels  62.4 us (97%)
  local copies, waits for them, and re-layouts  1.87 us (3%)
    pallas_call x1, Pallas kernels, on_device(): pl.pallas_call(kernel, out_shape=jax.ShapeDtypeStruct((rows, cols, C), BF...  62.4 us
    unnamed x1, local copies, waits for them, and re-layouts  1.87 us

profile of v1, /device:TPU:1, one launch (start us, length us, event | category | flops | bytes accessed | tf_op | source)
XLA Modules:
  0.0 64.2 jit_solution(17194840696515881179)
XLA Ops:
  0.0 62.4 %swin_pair.1 = bf16[8,256,128]{2,1,0:T(8,128)(2,1)} custom-call(bf16[8,256,128]{2,1,0:T(8,128)(2,1)} %x_in.1, s32[8,256]{1,0:T(8,128)} %lab_in.1, s32[64,64]{1,0:T(8,128)} %rel_in.1, f32[2,2,128]{2,1,0:T(2,128)} %gain_in.1, f32[2,2,128]{2,1,0:T(2,128)} %shift_in.1, bf16[2,3,64,128]{3,2,1,0:T(8,128)(2,1)} %bitcast.3, f32[3,2,64]{2,1,0:T(2,128)} %bitcast.5, ...), custom_call_target="tpu_custom_call" | custom-call | tf_op jit(solution)/shard_map/swin_pair/pallas_call | solution.py:433
  62.4 1.9 %copy.16 = bf16[8,256,128]{2,1,0:T(8,128)(2,1)} copy(bf16[8,256,128]{2,1,0:T(8,128)(2,1)} %swin_pair.1) | data formatting | bytes 1048576

commit v2 on v1

--- a/solution.py
+++ b/solution.py
@@ -39,10 +39,6 @@
 
 def dot_rows(a, b):
     return lax.dot_general(a, b, (((1,), (1,)), ((), ())), preferred_element_type=F32)
-
-
-def dot_first(a, b):
-    return lax.dot_general(a, b, (((0,), (0,)), ((), ())), preferred_element_type=F32)
 
 
 def kernel(
@@ -147,10 +143,8 @@
     heads = [(head_of == h).astype(F32).astype(BF) for h in range(HEADS)]
 
     entries = tbl.shape[-1]
-    relt = rel[...].astype(F32).T
 
     def lookup(index, side, b, h):
-        index = index.astype(jnp.int32)
         line = tbl[side, b, h : h + 1, :]
         a0 = jnp.broadcast_to(line[:, 0:128], index.shape)
         a1 = jnp.concatenate([line[:, 128:], jnp.zeros((1, 256 - entries), F32)], axis=1)
@@ -160,12 +154,10 @@
         g1 = jnp.take_along_axis(a1, within, axis=1)
         return jnp.where(index < 128, g0, g1) * LOG2E
 
-    twice = jnp.concatenate([relt, relt], axis=1)
-
     def first_bias(side):
-        bias0[:, 128 * side : 128 * side + 128] = jnp.where(
-            lane < 64, lookup(twice, side, 0, 0), lookup(twice, side, 0, 1)
-        )
+        twice = jnp.concatenate([rel[...], rel[...]], axis=1)
+        for h in range(2):
+            bias0[side, 64 * h : 64 * h + 64] = lookup(twice, side, 0, h)
 
     def zero_padded(values, side):
         pad = jnp.zeros_like(values)
@@ -182,15 +174,19 @@
         v = (r[:, 256:384] + bqkv[b, 2:3]).astype(BF)
         return q, k, v
 
-    def softmax(s):
-        raised = jnp.exp2(s - jnp.max(s, axis=0, keepdims=True))
-        return (raised * (1.0 / jnp.sum(raised, axis=0, keepdims=True))).astype(BF)
+    ones = jnp.ones((64, C), BF)
+
+    def weighted(s, values, each):
+        raised = jnp.exp2(s - jnp.max(s, axis=1, keepdims=True)).astype(BF)
+        o = dot(raised, jnp.concatenate([values, ones], axis=1))
+        return [(o[i : i + each, 0:C], o[i : i + each, C:]) for i in range(0, s.shape[0], each)]
 
     def half_attention(side, q, k, v):
         stacked = jnp.concatenate([q * heads[2 * side], q * heads[2 * side + 1]], axis=0)
-        s = dot_rows(k, stacked) + bias0[:, 128 * side : 128 * side + 128]
-        o = dot_first(softmax(s), v)
-        return jnp.where(head_of == 2 * side, o[0:64], o[64:128]).astype(BF)
+        s = dot_rows(stacked, k) + bias0[side, :, 0:64]
+        (o0, l0), (o1, l1) = weighted(s, v, 64)
+        here = head_of == 2 * side
+        return (jnp.where(here, o0, o1) * (1.0 / jnp.where(here, l0, l1))).astype(BF)
 
     def windows_of(base):
         lines = [x[r, pl.ds(base, CHUNK), :].astype(F32) for r in range(WIN)]
@@ -234,14 +230,12 @@
     for m in range(3):
         bqkv[1, m : m + 1] = zero_padded(qkvb[1, m, 0:1], 1)
         bqkv[2, m : m + 1] = jnp.concatenate([qkvb[0, m, 1:2], qkvb[1, m, 1:2]], axis=1)
-    for t, turned in enumerate(
-        (relt[:, 0:32], jnp.concatenate([relt[32:64, 32:64], relt[0:32, 32:64]], axis=0))
+    for t, part in enumerate(
+        (rel[0:32], jnp.concatenate([rel[32:64, 32:64], rel[32:64, 0:32]], axis=1))
     ):
-        index = jnp.concatenate([turned] * 4, axis=1)
-        picked = lookup(index, 1, 1, 1)
-        for h in (2, 1, 0):
-            picked = jnp.where(head_of == h, lookup(index, h // 2, 1, h % 2), picked)
-        bias1[t] = picked
+        index = jnp.concatenate([part, part], axis=1)
+        for h in range(HEADS):
+            bias1[t, 32 * h : 32 * h + 32] = lookup(index, h // 2, 1, h % 2)
 
     def feed(b, attended, tokens):
         mid = (tokens + dot(attended, wproj[b]) + projb[b : b + 1]).astype(BF).astype(F32)
@@ -376,14 +370,15 @@
                 keys = jnp.concatenate([k[at], k2[at]], axis=0)
                 values = jnp.concatenate([v[at], v2[at]], axis=0)
                 stacked = jnp.concatenate([q[at] * m for m in heads], axis=0)
-                s = dot_rows(keys, stacked) + bias1[1 - is_bottom]
-                key_id = jnp.concatenate(own_id[g] + beside_id[g], axis=0)
-                query_id = jnp.concatenate(own_id[g] * 4, axis=0).T[0:8]
-                allowed = key_id == jnp.concatenate([query_id] * 8, axis=0)
-                o = dot_first(softmax(jnp.where(allowed, s, EXCLUDED)), values)
-                mixed = o[96:128]
+                s = dot_rows(stacked, keys) + bias1[1 - is_bottom, :, 0:64]
+                key_id = jnp.concatenate(own_id[g] + beside_id[g], axis=0).T[0:8]
+                allowed = jnp.concatenate([i[:, 0:64] == key_id for i in own_id[g]] * 4, axis=0)
+                parts = weighted(jnp.where(allowed, s, EXCLUDED), values, 32)
+                mixed, total = parts[3]
                 for h in (2, 1, 0):
-                    mixed = jnp.where(head_of == h, o[32 * h : 32 * h + 32], mixed)
+                    mixed = jnp.where(head_of == h, parts[h][0], mixed)
+                    total = jnp.where(head_of == h, parts[h][1], total)
+                mixed = mixed * (1.0 / total)
                 attended.append(mixed.astype(BF))
             done = feed(1, jnp.concatenate(attended, axis=0), tokens)
             for g in range(span):
@@ -442,7 +437,7 @@
             like(fc1_weight, 2), like(fc1_bias, 2), like(fc2_weight, 2), like(fc2_bias),
             V((3, C, C), BF), V((3, C, C), BF), V((3, C, C), BF),
             V((3, 3, C), F32),
-            V((64, 256), F32), V((2, 64, C), F32),
+            V((2, C, C), F32), V((2, C, C), F32),
             V((2 * WIN, cols + 8, C), F32), V((2 * WIN, cols + 8, C), F32),
             V((rows * cols, C), BF), V((rows * cols, C), BF),
             V((rows, cols, C), BF),

time: 64.4 us -> 55 us (0.85)
  Pallas kernels: 62.4 us -> 53 us
    pallas_call x1, Pallas kernels: 62.4 us -> 53 us  [on_device(): pl.pallas_call(kernel, out_shape=jax.ShapeDtypeStruct((rows, cols, C), BF...]
where the time goes in v2:
time: 55 us; the launch traced here: 54.8 us
  Pallas kernels  53 us (96%)
  local copies, waits for them, and re-layouts  1.87 us (3%)
    pallas_call x1, Pallas kernels, on_device(): pl.pallas_call(kernel, out_shape=jax.ShapeDtypeStruct((rows, cols, C), BF...  53 us
    unnamed x1, local copies, waits for them, and re-layouts  1.87 us

profile of v2, /device:TPU:1, one launch (start us, length us, event | category | flops | bytes accessed | tf_op | source)
XLA Modules:
  0.0 54.8 jit_solution(5946979699757986157)
XLA Ops:
  0.0 53.0 %swin_pair.1 = bf16[8,256,128]{2,1,0:T(8,128)(2,1)} custom-call(bf16[8,256,128]{2,1,0:T(8,128)(2,1)} %x_in.1, s32[8,256]{1,0:T(8,128)} %lab_in.1, s32[64,64]{1,0:T(8,128)} %rel_in.1, f32[2,2,128]{2,1,0:T(2,128)} %gain_in.1, f32[2,2,128]{2,1,0:T(2,128)} %shift_in.1, bf16[2,3,64,128]{3,2,1,0:T(8,128)(2,1)} %bitcast.3, f32[3,2,64]{2,1,0:T(2,128)} %bitcast.5, ...), custom_call_target="tpu_custom_call" | custom-call | tf_op jit(solution)/shard_map/swin_pair/pallas_call | solution.py:428
  53.0 1.9 %copy.16 = bf16[8,256,128]{2,1,0:T(8,128)(2,1)} copy(bf16[8,256,128]{2,1,0:T(8,128)(2,1)} %swin_pair.1) | data formatting | bytes 1048576

commit v3 on v2

--- a/solution.py
+++ b/solution.py
@@ -24,6 +24,7 @@
 
 GROUP = 8
 CHUNK = GROUP * WIN
+PACK = 2
 SPANS = 3
 
 
@@ -68,12 +69,13 @@
         return {"row": b // groups, "col": c, "ch": lax.rem(b, groups)}
 
     partner = {"row": lax.axis_index("row"), "col": col, "ch": 1 - ch}
+    across = {"row": lax.axis_index("row"), "col": lax.rem(col + tiles // 2, tiles), "ch": 1 - ch}
     up, down = device(-1, 0), device(1, 0)
     left, right = device(0, -1), device(0, 1)
     diagonals = [device(i, j) for i in (-1, 1) for j in (-1, 1)]
 
     barrier = pltpu.get_barrier_semaphore()
-    peers = [up, down, left, right] + diagonals
+    peers = [up, down, left, right, across] + diagonals
     for peer in peers:
         pl.semaphore_signal(barrier, inc=1, device_id=peer, device_id_type=MESH)
 
@@ -121,17 +123,25 @@
     ]
     def feed_copies(b):
         return [
-            copy(4 + 4 * b, wproj.at[b, own_rows], wproj.at[b, other_rows], partner),
-            copy(5 + 4 * b, w1.at[0, b], w1.at[1, b], partner),
-            copy(6 + 4 * b, w2.at[0, b], w2.at[1, b], partner),
+            copy(4 + 4 * b, wproj.at[b, own_rows], wproj.at[b, other_rows], across),
+            copy(5 + 4 * b, w1.at[0, b], w1.at[1, b], across),
+            copy(6 + 4 * b, w2.at[0, b], w2.at[1, b], across),
         ]
     second = feed_copies(0)
-    third = [copy(7, wfull.at[:, own_rows], wfull.at[:, other_rows], partner)] + feed_copies(1)
+    third = [copy(7, wfull.at[:, own_rows], wfull.at[:, other_rows], across)] + feed_copies(1)
     half_at = {-1: pl.ds(0, 128), 1: pl.ds(cols - 128, 128)}
-    region_copies = [copy(11, region, labs.at[0], up), copy(12, region, labs.at[1], down)] + [
-        copy(13 + i, region.at[:, half_at[side]], labs.at[2 + i, :, pl.ds(0, 128)], to)
-        for i, (side, to) in enumerate(
-            [(-1, left), (1, right)] + list(zip((-1, 1, -1, 1), diagonals))
+    region_copies = [
+        copy(11, region.at[pl.ds(0, SHIFT)], labs.at[0, pl.ds(0, SHIFT)], up),
+        copy(12, region.at[pl.ds(SHIFT, SHIFT)], labs.at[1, pl.ds(SHIFT, SHIFT)], down),
+        copy(13, region.at[:, half_at[-1]], labs.at[2, :, pl.ds(0, 128)], left),
+        copy(14, region.at[:, half_at[1]], labs.at[3, :, pl.ds(0, 128)], right),
+    ] + [
+        copy(
+            15 + i, region.at[pl.ds(r0, SHIFT), half_at[side]],
+            labs.at[4 + i, pl.ds(r0, SHIFT), pl.ds(0, 128)], to,
+        )
+        for i, ((r0, side), to) in enumerate(
+            zip(((0, -1), (0, 1), (SHIFT, -1), (SHIFT, 1)), diagonals)
         )
     ]
 
@@ -154,10 +164,14 @@
         g1 = jnp.take_along_axis(a1, within, axis=1)
         return jnp.where(index < 128, g0, g1) * LOG2E
 
+    def put_bias(bias, i, rows, values):
+        bias[i, 0, rows] = jnp.where(lane < 64, values, EXCLUDED)
+        bias[i, 1, rows] = jnp.where(lane < 64, EXCLUDED, values)
+
     def first_bias(side):
         twice = jnp.concatenate([rel[...], rel[...]], axis=1)
         for h in range(2):
-            bias0[side, 64 * h : 64 * h + 64] = lookup(twice, side, 0, h)
+            put_bias(bias0, side, slice(64 * h, 64 * h + 64), lookup(twice, side, 0, h))
 
     def zero_padded(values, side):
         pad = jnp.zeros_like(values)
@@ -174,19 +188,36 @@
         v = (r[:, 256:384] + bqkv[b, 2:3]).astype(BF)
         return q, k, v
 
-    ones = jnp.ones((64, C), BF)
-
-    def weighted(s, values, each):
-        raised = jnp.exp2(s - jnp.max(s, axis=1, keepdims=True)).astype(BF)
-        o = dot(raised, jnp.concatenate([values, ones], axis=1))
-        return [(o[i : i + each, 0:C], o[i : i + each, C:]) for i in range(0, s.shape[0], each)]
+    def weighted(queries, keys, values, bias, allowed, each):
+        width = 64 * len(queries)
+        s = dot_rows(jnp.concatenate(queries, axis=0), jnp.concatenate(keys, axis=0))
+        s = [s[C * i : C * i + C] + bias[i, :, 0:width] for i in range(len(queries))]
+        if allowed is not None:
+            s = [jnp.where(a, b, EXCLUDED) for a, b in zip(allowed, s)]
+        raised = [jnp.exp2(a - jnp.max(a, axis=1, keepdims=True)) for a in s]
+        totals = [jnp.sum(a, axis=1, keepdims=True) for a in raised]
+        o = dot(
+            jnp.concatenate([a.astype(BF) for a in raised], axis=0),
+            jnp.concatenate(values, axis=0),
+        )
+        mixed = []
+        for i, total in enumerate(totals):
+            part = o[C * i : C * i + C] * (1.0 / total)
+            mixed.append([part[k : k + each] for k in range(0, C, each)])
+        return mixed
 
     def half_attention(side, q, k, v):
-        stacked = jnp.concatenate([q * heads[2 * side], q * heads[2 * side + 1]], axis=0)
-        s = dot_rows(stacked, k) + bias0[side, :, 0:64]
-        (o0, l0), (o1, l1) = weighted(s, v, 64)
-        here = head_of == 2 * side
-        return (jnp.where(here, o0, o1) * (1.0 / jnp.where(here, l0, l1))).astype(BF)
+        cut = lambda a: [a[64 * g : 64 * g + 64] for g in range(GROUP)]
+        stacked = [
+            jnp.concatenate([a * heads[2 * side], a * heads[2 * side + 1]], axis=0) for a in cut(q)
+        ]
+        k, v = cut(k), cut(v)
+        out = []
+        for g in range(0, GROUP, 2):
+            two = slice(g, g + 2)
+            for o0, o1 in weighted(stacked[two], k[two], v[two], bias0.at[side], None, 64):
+                out.append(jnp.where(head_of == 2 * side, o0, o1).astype(BF))
+        return jnp.concatenate(out, axis=0)
 
     def windows_of(base):
         lines = [x[r, pl.ds(base, CHUNK), :].astype(F32) for r in range(WIN)]
@@ -200,10 +231,7 @@
         n = norm(windows_of(base), gain[0, 0:1], shift[0, 0:1])
         normed[at, :] = n
         q, k, v = project(n, wown, 0)
-        att[at, :] = jnp.concatenate(
-            [half_attention(0, *(a[64 * g : 64 * g + 64] for a in (q, k, v))) for g in range(GROUP)],
-            axis=0,
-        )
+        att[at, :] = half_attention(0, q, k, v)
         return carry
 
     lax.fori_loop(0, chunks, own_heads, 0)
@@ -235,7 +263,7 @@
     ):
         index = jnp.concatenate([part, part], axis=1)
         for h in range(HEADS):
-            bias1[t, 32 * h : 32 * h + 32] = lookup(index, h // 2, 1, h % 2)
+            put_bias(bias1, t, slice(32 * h, 32 * h + 32), lookup(index, h // 2, 1, h % 2))
 
     def feed(b, attended, tokens):
         mid = (tokens + dot(attended, wproj[b]) + projb[b : b + 1]).astype(BF).astype(F32)
@@ -250,21 +278,19 @@
     for c in second:
         c.wait_recv()
 
-    def halo_copies(k):
+    def halo_copy(near, k):
         at = pl.ds(pl.multiple_of(k * CHUNK, CHUNK), CHUNK)
-        return (
-            copy(20 + k, halo.at[pl.ds(0, SHIFT), at], both.at[0, :, at], up),
-            copy(24 + k, halo.at[pl.ds(SHIFT, SHIFT), at], both.at[1, :, at], down),
+        to_down = 1 - ch if near else ch
+        return copy(
+            20 + 4 * to_down + k, halo.at[pl.ds(SHIFT * to_down, SHIFT), at],
+            both.at[to_down, :, at], partner if near else device(2 * ch - 1, 0),
         )
 
     def first_block(k, carry):
         base = pl.multiple_of(k * CHUNK, CHUNK)
         at = pl.ds(pl.multiple_of(k * 64 * GROUP, 64 * GROUP), 64 * GROUP)
         q, key, v = project(normed[at, :], woth, 1)
-        other = jnp.concatenate(
-            [half_attention(1, *(a[64 * g : 64 * g + 64] for a in (q, key, v))) for g in range(GROUP)],
-            axis=0,
-        )
+        other = half_attention(1, q, key, v)
         done = feed(0, att[at, :] + other, windows_of(base))
         for r in range(WIN):
             line = jnp.concatenate(
@@ -272,12 +298,13 @@
             )
             y[SHIFT + r, pl.ds(base + SHIFT, CHUNK), :] = line
             halo[r, pl.ds(base, CHUNK), :] = line.astype(BF)
-        for c in halo_copies(k):
-            c.start()
+        halo_copy(True, k).start()
         return carry
 
     lax.fori_loop(0, chunks, first_block, 0)
 
+    for k in range(chunks):
+        halo_copy(False, k).start()
     edge = {-1: pl.ds(0, 16), 1: pl.ds(cols - 16, 16)}
     edge_copies = [
         copy(28, halo.at[:, edge[-1]], sides.at[1], left),
@@ -365,21 +392,26 @@
             k2 = (r2[:, 0:128] + bqkv[2, 1:2]).astype(BF)
             v2 = (r2[:, 128:256] + bqkv[2, 2:3]).astype(BF)
             attended = []
-            for g in range(span):
-                at = slice(32 * g, 32 * g + 32)
-                keys = jnp.concatenate([k[at], k2[at]], axis=0)
-                values = jnp.concatenate([v[at], v2[at]], axis=0)
-                stacked = jnp.concatenate([q[at] * m for m in heads], axis=0)
-                s = dot_rows(stacked, keys) + bias1[1 - is_bottom, :, 0:64]
-                key_id = jnp.concatenate(own_id[g] + beside_id[g], axis=0).T[0:8]
-                allowed = jnp.concatenate([i[:, 0:64] == key_id for i in own_id[g]] * 4, axis=0)
-                parts = weighted(jnp.where(allowed, s, EXCLUDED), values, 32)
-                mixed, total = parts[3]
-                for h in (2, 1, 0):
-                    mixed = jnp.where(head_of == h, parts[h][0], mixed)
-                    total = jnp.where(head_of == h, parts[h][1], total)
-                mixed = mixed * (1.0 / total)
-                attended.append(mixed.astype(BF))
+            for first_window in range(0, span, PACK):
+                group = [min(first_window + i, span - 1) for i in range(PACK)]
+                queries, keys, values, key_ids = [], [], [], []
+                for g in group:
+                    at = slice(32 * g, 32 * g + 32)
+                    queries.append(jnp.concatenate([q[at] * m for m in heads], axis=0))
+                    keys.append(jnp.concatenate([k[at], k2[at]], axis=0))
+                    values.append(jnp.concatenate([v[at], v2[at]], axis=0))
+                    key_ids += own_id[g] + beside_id[g]
+                key_id = jnp.concatenate(key_ids, axis=0).T[0:8]
+                width = 64 * len(group)
+                allowed = [
+                    jnp.concatenate([i[:, 0:width] == key_id for i in own_id[g]] * 4, axis=0)
+                    for g in group
+                ]
+                for parts in weighted(queries, keys, values, bias1.at[1 - is_bottom], allowed, 32)[: span - first_window]:
+                    mixed = parts[3]
+                    for h in (2, 1, 0):
+                        mixed = jnp.where(head_of == h, parts[h], mixed)
+                    attended.append(mixed.astype(BF))
             done = feed(1, jnp.concatenate(attended, axis=0), tokens)
             for g in range(span):
                 for r in range(SHIFT):
@@ -407,8 +439,8 @@
     for c in first + second + third + region_copies + edge_copies:
         c.wait_send()
     for k in range(chunks):
-        for c in halo_copies(k):
-            c.wait_send()
+        for near in (True, False):
+            halo_copy(near, k).wait_send()
 
 
 def on_device(
@@ -437,7 +469,7 @@
             like(fc1_weight, 2), like(fc1_bias, 2), like(fc2_weight, 2), like(fc2_bias),
             V((3, C, C), BF), V((3, C, C), BF), V((3, C, C), BF),
             V((3, 3, C), F32),
-            V((2, C, C), F32), V((2, C, C), F32),
+            V((2, PACK, C, C), F32), V((2, PACK, C, C), F32),
             V((2 * WIN, cols + 8, C), F32), V((2 * WIN, cols + 8, C), F32),
             V((rows * cols, C), BF), V((rows * cols, C), BF),
             V((rows, cols, C), BF),

time: 55 us -> 46.3 us (0.84)
  the two profiles are of different devices: /device:TPU:1 before, /device:TPU:9 now
where the time goes in v3:
time: 46.3 us; the launch traced here: 46.2 us
  Pallas kernels  44.3 us (96%)
  local copies, waits for them, and re-layouts  1.87 us (4%)
    pallas_call x1, Pallas kernels, on_device(): pl.pallas_call(kernel, out_shape=jax.ShapeDtypeStruct((rows, cols, C), BF...  44.3 us
    unnamed x1, local copies, waits for them, and re-layouts  1.87 us

profile of v3, /device:TPU:9, one launch (start us, length us, event | category | flops | bytes accessed | tf_op | source)
XLA Modules:
  0.0 46.2 jit_solution(10652299386983538420)
XLA Ops:
  0.0 44.3 %swin_pair.1 = bf16[8,256,128]{2,1,0:T(8,128)(2,1)} custom-call(bf16[8,256,128]{2,1,0:T(8,128)(2,1)} %x_in.1, s32[8,256]{1,0:T(8,128)} %lab_in.1, s32[64,64]{1,0:T(8,128)} %rel_in.1, f32[2,2,128]{2,1,0:T(2,128)} %gain_in.1, f32[2,2,128]{2,1,0:T(2,128)} %shift_in.1, bf16[2,3,64,128]{3,2,1,0:T(8,128)(2,1)} %bitcast.3, f32[3,2,64]{2,1,0:T(2,128)} %bitcast.5, ...), custom_call_target="tpu_custom_call" | custom-call | tf_op jit(solution)/shard_map/swin_pair/pallas_call | solution.py:460
  44.3 1.9 %copy.16 = bf16[8,256,128]{2,1,0:T(8,128)(2,1)} copy(bf16[8,256,128]{2,1,0:T(8,128)(2,1)} %swin_pair.1) | data formatting | bytes 1048576

commit v4 on v3

--- a/solution.py
+++ b/solution.py
@@ -48,7 +48,7 @@
     out_ref,
     x, lab, rel, gain, shift, qkvb, tbl, wproj, projb, w1, b1, w2, fc2b,
     wown, woth, wfull, bqkv, bias0, bias1,
-    y, ids, normed, att, result, region, labs,
+    y, ids, normed, att, region, labs,
     halo, both, sides, corners,
     local, send, recv,
 ):
@@ -124,7 +124,7 @@
     def feed_copies(b):
         return [
             copy(4 + 4 * b, wproj.at[b, own_rows], wproj.at[b, other_rows], across),
-            copy(5 + 4 * b, w1.at[0, b], w1.at[1, b], across),
+            copy(5 + 4 * b, w1.at[0, b], w1.at[1, b], (partner, across)[b]),
             copy(6 + 4 * b, w2.at[0, b], w2.at[1, b], across),
         ]
     second = feed_copies(0)
@@ -225,7 +225,25 @@
             [lines[r][WIN * g : WIN * g + WIN] for g in range(GROUP) for r in range(WIN)], axis=0
         )
 
+    def meet():
+        for c in late:
+            c.wait()
+        i = lax.broadcasted_iota(jnp.int32, lab.shape, 0)
+        j = lax.broadcasted_iota(jnp.int32, lab.shape, 1)
+        first_band = (band == 0).astype(jnp.int32)
+        first_tile = (col == 0).astype(jnp.int32)
+        region[...] = (
+            lab[...] * 4
+            + (i < SHIFT).astype(jnp.int32) * (2 * first_band)
+            + (j < SHIFT).astype(jnp.int32) * first_tile
+        )
+
+        pl.semaphore_wait(barrier, len(peers))
+        for c in first + second + third + region_copies:
+            c.start()
+
     def own_heads(j, carry):
+        pl.when(j == 1)(meet)
         base = pl.multiple_of(j * CHUNK, CHUNK)
         at = pl.ds(pl.multiple_of(j * 64 * GROUP, 64 * GROUP), 64 * GROUP)
         n = norm(windows_of(base), gain[0, 0:1], shift[0, 0:1])
@@ -235,22 +253,6 @@
         return carry
 
     lax.fori_loop(0, chunks, own_heads, 0)
-
-    for c in late:
-        c.wait()
-    i = lax.broadcasted_iota(jnp.int32, lab.shape, 0)
-    j = lax.broadcasted_iota(jnp.int32, lab.shape, 1)
-    first_band = (band == 0).astype(jnp.int32)
-    first_tile = (col == 0).astype(jnp.int32)
-    region[...] = (
-        lab[...] * 4
-        + (i < SHIFT).astype(jnp.int32) * (2 * first_band)
-        + (j < SHIFT).astype(jnp.int32) * first_tile
-    )
-
-    pl.semaphore_wait(barrier, len(peers))
-    for c in first + second + region_copies + third:
-        c.start()
 
     for c in first:
         c.wait_recv()
@@ -286,7 +288,24 @@
             both.at[to_down, :, at], partner if near else device(2 * ch - 1, 0),
         )
 
-    def first_block(k, carry):
+    edge = {-1: pl.ds(0, 16), 1: pl.ds(cols - 16, 16)}
+    side_copies = [
+        copy(28, halo.at[:, edge[-1]], sides.at[1], left),
+        copy(29, halo.at[:, edge[1]], sides.at[0], right),
+    ]
+
+    def corner_copies(near):
+        to_down = 1 - ch if near else ch
+        return [
+            copy(
+                30 + 2 * to_down + i, halo.at[pl.ds(SHIFT * to_down, SHIFT), edge[side]],
+                corners.at[2 * to_down + i], device(2 * to_down - 1, side),
+            )
+            for i, side in enumerate((-1, 1))
+        ]
+
+    def first_block(step, carry):
+        k = lax.rem(step + chunks - 1, chunks)
         base = pl.multiple_of(k * CHUNK, CHUNK)
         at = pl.ds(pl.multiple_of(k * 64 * GROUP, 64 * GROUP), 64 * GROUP)
         q, key, v = project(normed[at, :], woth, 1)
@@ -299,23 +318,19 @@
             y[SHIFT + r, pl.ds(base + SHIFT, CHUNK), :] = line
             halo[r, pl.ds(base, CHUNK), :] = line.astype(BF)
         halo_copy(True, k).start()
+
+        @pl.when(step == 1)
+        def _():
+            for c in side_copies + corner_copies(True):
+                c.start()
+
         return carry
 
     lax.fori_loop(0, chunks, first_block, 0)
 
     for k in range(chunks):
         halo_copy(False, k).start()
-    edge = {-1: pl.ds(0, 16), 1: pl.ds(cols - 16, 16)}
-    edge_copies = [
-        copy(28, halo.at[:, edge[-1]], sides.at[1], left),
-        copy(29, halo.at[:, edge[1]], sides.at[0], right),
-    ] + [
-        copy(30 + i, halo.at[pl.ds(r0, SHIFT), edge[side]], corners.at[i], to)
-        for i, ((r0, side), to) in enumerate(
-            zip(((0, -1), (0, 1), (SHIFT, -1), (SHIFT, 1)), diagonals)
-        )
-    ]
-    for c in edge_copies:
+    for c in corner_copies(False):
         c.start()
 
     for c in region_copies:
@@ -340,7 +355,7 @@
 
     for c in third:
         c.wait_recv()
-    for c in edge_copies[0:2]:
+    for c in side_copies:
         c.wait_recv()
     ends = ((slice(0, SHIFT), slice(12, 16)), (slice(SHIFT + cols, 2 * SHIFT + cols), slice(0, SHIFT)))
     for s, (to, of) in enumerate(ends):
@@ -422,25 +437,19 @@
         lax.fori_loop(0, SPANS, body, 0)
         row = SHIFT * is_bottom
         for r in range(SHIFT):
-            result[row + r] = y[mine + r, SHIFT : SHIFT + cols, :].astype(BF)
-        return pltpu.make_async_copy(
-            result.at[pl.ds(row, SHIFT)], out_ref.at[pl.ds(row, SHIFT)], local.at[15 + is_bottom]
-        )
+            out_ref[row + r] = y[mine + r, SHIFT : SHIFT + cols, :].astype(BF)
 
     near = 1 - ch
-    outs = []
-    for is_bottom in (near, 1 - near):
-        c = shifted_band(is_bottom)
-        c.start()
-        outs.append(c)
-    for c in outs:
-        c.wait()
-
-    for c in first + second + third + region_copies + edge_copies:
+    shifted_band(near)
+    shifted_band(1 - near)
+
+    for c in first + second + third + region_copies + side_copies:
         c.wait_send()
     for k in range(chunks):
         for near in (True, False):
             halo_copy(near, k).wait_send()
+    for c in corner_copies(True) + corner_copies(False):
+        c.wait_send()
 
 
 def on_device(
@@ -459,9 +468,9 @@
     copies = 34
     return pl.pallas_call(
         kernel,
-        out_shape=jax.ShapeDtypeStruct((rows, cols, C), BF),
+        out_shape=pltpu.VMEM((rows, cols, C), BF),
         in_specs=[pl.BlockSpec(memory_space=pl.ANY)] * len(args),
-        out_specs=pl.BlockSpec(memory_space=pl.ANY),
+        out_specs=pl.BlockSpec(memory_space=pltpu.VMEM),
         scratch_shapes=[
             like(image_tokens), like(labels), like(rel_index), like(norm_gain), like(norm_shift),
             like(args[6], 2), like(args[7], 2),
@@ -472,11 +481,10 @@
             V((2, PACK, C, C), F32), V((2, PACK, C, C), F32),
             V((2 * WIN, cols + 8, C), F32), V((2 * WIN, cols + 8, C), F32),
             V((rows * cols, C), BF), V((rows * cols, C), BF),
-            V((rows, cols, C), BF),
             like(labels), like(labels, 8),
             V((rows, cols, C), BF), V((2, SHIFT, cols, C), BF),
             V((2, rows, 16, C), BF), V((4, SHIFT, 16, C), BF),
-            pltpu.SemaphoreType.DMA((17,)),
+            pltpu.SemaphoreType.DMA((15,)),
             pltpu.SemaphoreType.DMA((copies,)),
             pltpu.SemaphoreType.DMA((copies,)),
         ],

time: 46.3 us -> 42.3 us (0.914)
  the two profiles are of different devices: /device:TPU:9 before, /device:TPU:1 now
where the time goes in v4:
time: 42.3 us; the launch traced here: 42.2 us
  Pallas kernels  41.4 us (98%)
  local copies, waits for them, and re-layouts  0.8 us (2%)
    pallas_call x1, Pallas kernels, on_device(): pl.pallas_call(kernel, out_shape=pltpu.VMEM((rows, cols, C), BF), in_spec...  41.4 us

profile of v4, /device:TPU:1, one launch (start us, length us, event | category | flops | bytes accessed | tf_op | source)
XLA Modules:
  0.0 42.2 jit_solution(17197901273411760822)
XLA Ops:
  0.0 41.4 %swin_pair.1 = bf16[8,256,128]{2,1,0:T(8,128)(2,1)S(1)} custom-call(bf16[8,256,128]{2,1,0:T(8,128)(2,1)} %x_in.1, s32[8,256]{1,0:T(8,128)} %lab_in.1, s32[64,64]{1,0:T(8,128)} %rel_in.1, f32[2,2,128]{2,1,0:T(2,128)} %gain_in.1, f32[2,2,128]{2,1,0:T(2,128)} %shift_in.1, bf16[2,3,64,128]{3,2,1,0:T(8,128)(2,1)} %bitcast.3, f32[3,2,64]{2,1,0:T(2,128)} %bitcast.5, ...), custom_call_target="tpu_custom_call" | custom-call | tf_op jit(solution)/shard_map/swin_pair/pallas_call | solution.py:469
  41.4 0.8 %copy.16 = bf16[8,256,128]{2,1,0:T(8,128)(2,1)} copy(bf16[8,256,128]{2,1,0:T(8,128)(2,1)S(1)} %swin_pair.1) | data formatting | bytes 1048576

commit v5 on v4

--- a/solution.py
+++ b/solution.py
@@ -48,9 +48,9 @@
     out_ref,
     x, lab, rel, gain, shift, qkvb, tbl, wproj, projb, w1, b1, w2, fc2b,
     wown, woth, wfull, bqkv, bias0, bias1,
-    y, ids, normed, att, region, labs,
+    y, ids, normed, att, region, lab_row, lab_side, lab_corner,
     halo, both, sides, corners,
-    local, send, recv,
+    ready, local, send, recv,
 ):
     cols = x.shape[1]
     chunks = cols // CHUNK
@@ -72,12 +72,21 @@
     across = {"row": lax.axis_index("row"), "col": lax.rem(col + tiles // 2, tiles), "ch": 1 - ch}
     up, down = device(-1, 0), device(1, 0)
     left, right = device(0, -1), device(0, 1)
-    diagonals = [device(i, j) for i in (-1, 1) for j in (-1, 1)]
+
+    def towards(near):
+        to_down = 1 - ch if near else ch
+        return to_down, [device(2 * to_down - 1, side) for side in (0, -1, 1)]
 
     barrier = pltpu.get_barrier_semaphore()
-    peers = [up, down, left, right, across] + diagonals
-    for peer in peers:
-        pl.semaphore_signal(barrier, inc=1, device_id=peer, device_id_type=MESH)
+    peers = [left, right, across] + towards(True)[1]
+    strangers = towards(False)[1]
+
+    def greet(semaphore, devices):
+        for to in devices:
+            pl.semaphore_signal(semaphore, inc=1, device_id=to, device_id_type=MESH)
+
+    greet(barrier, peers)
+    pl.when(ch == 0)(lambda: greet(barrier, strangers))
 
     def load(i, src, dst):
         return pltpu.make_async_copy(src, dst, local.at[i])
@@ -130,20 +139,20 @@
     second = feed_copies(0)
     third = [copy(7, wfull.at[:, own_rows], wfull.at[:, other_rows], across)] + feed_copies(1)
     half_at = {-1: pl.ds(0, 128), 1: pl.ds(cols - 128, 128)}
-    region_copies = [
-        copy(11, region.at[pl.ds(0, SHIFT)], labs.at[0, pl.ds(0, SHIFT)], up),
-        copy(12, region.at[pl.ds(SHIFT, SHIFT)], labs.at[1, pl.ds(SHIFT, SHIFT)], down),
-        copy(13, region.at[:, half_at[-1]], labs.at[2, :, pl.ds(0, 128)], left),
-        copy(14, region.at[:, half_at[1]], labs.at[3, :, pl.ds(0, 128)], right),
-    ] + [
-        copy(
-            15 + i, region.at[pl.ds(r0, SHIFT), half_at[side]],
-            labs.at[4 + i, pl.ds(r0, SHIFT), pl.ds(0, 128)], to,
-        )
-        for i, ((r0, side), to) in enumerate(
-            zip(((0, -1), (0, 1), (SHIFT, -1), (SHIFT, 1)), diagonals)
-        )
+    side_regions = [
+        copy(13, region.at[:, :, half_at[-1]], lab_side.at[1], left),
+        copy(14, region.at[:, :, half_at[1]], lab_side.at[0], right),
     ]
+
+    def band_regions(near):
+        to_down, (to, *diagonals) = towards(near)
+        return [copy(11 + to_down, region.at[to_down], lab_row.at[to_down], to)] + [
+            copy(
+                15 + 2 * to_down + i, region.at[to_down, :, half_at[side]],
+                lab_corner.at[2 * to_down + i], diagonals[i],
+            )
+            for i, side in enumerate((-1, 1))
+        ]
 
     for c in early:
         c.wait()
@@ -232,14 +241,17 @@
         j = lax.broadcasted_iota(jnp.int32, lab.shape, 1)
         first_band = (band == 0).astype(jnp.int32)
         first_tile = (col == 0).astype(jnp.int32)
-        region[...] = (
+        regions = (
             lab[...] * 4
             + (i < SHIFT).astype(jnp.int32) * (2 * first_band)
             + (j < SHIFT).astype(jnp.int32) * first_tile
         )
-
-        pl.semaphore_wait(barrier, len(peers))
-        for c in first + second + third + region_copies:
+        for half in range(2):
+            region[half] = regions[SHIFT * half : SHIFT * half + SHIFT]
+
+        pl.semaphore_wait(barrier, len(peers) + len(strangers) * ch)
+        pl.when(ch == 1)(lambda: greet(ready, strangers))
+        for c in first + second + third + side_regions + band_regions(True):
             c.start()
 
     def own_heads(j, carry):
@@ -282,10 +294,10 @@
 
     def halo_copy(near, k):
         at = pl.ds(pl.multiple_of(k * CHUNK, CHUNK), CHUNK)
-        to_down = 1 - ch if near else ch
+        to_down = towards(near)[0]
         return copy(
             20 + 4 * to_down + k, halo.at[pl.ds(SHIFT * to_down, SHIFT), at],
-            both.at[to_down, :, at], partner if near else device(2 * ch - 1, 0),
+            both.at[to_down, :, at], towards(near)[1][0],
         )
 
     edge = {-1: pl.ds(0, 16), 1: pl.ds(cols - 16, 16)}
@@ -295,11 +307,11 @@
     ]
 
     def corner_copies(near):
-        to_down = 1 - ch if near else ch
+        to_down, (_, *diagonals) = towards(near)
         return [
             copy(
                 30 + 2 * to_down + i, halo.at[pl.ds(SHIFT * to_down, SHIFT), edge[side]],
-                corners.at[2 * to_down + i], device(2 * to_down - 1, side),
+                corners.at[2 * to_down + i], diagonals[i],
             )
             for i, side in enumerate((-1, 1))
         ]
@@ -328,30 +340,33 @@
 
     lax.fori_loop(0, chunks, first_block, 0)
 
+    pl.when(ch == 0)(lambda: pl.semaphore_wait(ready, len(strangers)))
+    for c in band_regions(False):
+        c.start()
     for k in range(chunks):
         halo_copy(False, k).start()
     for c in corner_copies(False):
         c.start()
 
-    for c in region_copies:
-        c.wait_recv()
-
     def spread(line):
         return jnp.broadcast_to(line.astype(F32), (128, 128)).T
 
-    for r in range(2 * WIN):
-        if r < SHIFT:
-            middle, before, after, at = labs.at[1], labs.at[7], labs.at[6], SHIFT + r
-        elif r < SHIFT + WIN:
-            middle, before, after, at = region, labs.at[3], labs.at[2], r - SHIFT
-        else:
-            middle, before, after, at = labs.at[0], labs.at[5], labs.at[4], r - SHIFT - WIN
-        for t in range(cols // 128):
-            ids[r, SHIFT + 128 * t : SHIFT + 128 * t + 128, :] = spread(
-                middle[at : at + 1, 128 * t : 128 * t + 128]
-            )
-        ids[r, 0:SHIFT, :] = spread(before[at : at + 1, 0:128])[128 - SHIFT :]
-        ids[r, SHIFT + cols : 2 * SHIFT + cols, :] = spread(after[at : at + 1, 0:128])[0:SHIFT]
+    def put_ids(row, middle, before, after):
+        for r in range(SHIFT):
+            line = slice(r, r + 1)
+            for t in range(cols // 128):
+                ids[row + r, SHIFT + 128 * t : SHIFT + 128 * t + 128, :] = spread(
+                    middle[line, 128 * t : 128 * t + 128]
+                )
+            ids[row + r, 0:SHIFT, :] = spread(before[line])[128 - SHIFT :]
+            ids[row + r, SHIFT + cols : 2 * SHIFT + cols, :] = spread(after[line])[0:SHIFT]
+
+    for c in side_regions:
+        c.wait_recv()
+    for half in range(2):
+        put_ids(
+            SHIFT + SHIFT * half, region.at[half], lab_side.at[0, half], lab_side.at[1, half]
+        )
 
     for c in third:
         c.wait_recv()
@@ -375,7 +390,13 @@
             for r in range(SHIFT):
                 y[theirs + r, pl.ds(k * CHUNK + SHIFT, CHUNK), :] = arrived[r, at, :].astype(F32)
 
-        corner = 2 * (1 - is_bottom)
+        above = 1 - is_bottom
+        corner = 2 * above
+        copy(11 + above, lab_row.at[above], lab_row.at[above], up).wait_recv()
+        for i in range(2):
+            part = lab_corner.at[corner + i]
+            copy(15 + corner + i, part, part, up).wait_recv()
+        put_ids(theirs, lab_row.at[above], lab_corner.at[corner + 1], lab_corner.at[corner])
         for i in range(2):
             part = corners.at[corner + i]
             copy(30 + corner + i, part, part, up).wait_recv()
@@ -439,17 +460,17 @@
         for r in range(SHIFT):
             out_ref[row + r] = y[mine + r, SHIFT : SHIFT + cols, :].astype(BF)
 
-    near = 1 - ch
-    shifted_band(near)
-    shifted_band(1 - near)
-
-    for c in first + second + third + region_copies + side_copies:
+    shifted_band(1 - ch)
+    shifted_band(ch)
+
+    for c in first + second + third + side_regions + side_copies:
         c.wait_send()
     for k in range(chunks):
         for near in (True, False):
             halo_copy(near, k).wait_send()
-    for c in corner_copies(True) + corner_copies(False):
-        c.wait_send()
+    for near in (True, False):
+        for c in corner_copies(near) + band_regions(near):
+            c.wait_send()
 
 
 def on_device(
@@ -481,9 +502,11 @@
             V((2, PACK, C, C), F32), V((2, PACK, C, C), F32),
             V((2 * WIN, cols + 8, C), F32), V((2 * WIN, cols + 8, C), F32),
             V((rows * cols, C), BF), V((rows * cols, C), BF),
-            like(labels), like(labels, 8),
+            V((2, SHIFT, cols), jnp.int32), V((2, SHIFT, cols), jnp.int32),
+            V((2, 2, SHIFT, 128), jnp.int32), V((4, SHIFT, 128), jnp.int32),
             V((rows, cols, C), BF), V((2, SHIFT, cols, C), BF),
             V((2, rows, 16, C), BF), V((4, SHIFT, 16, C), BF),
+            pltpu.SemaphoreType.REGULAR,
             pltpu.SemaphoreType.DMA((15,)),
             pltpu.SemaphoreType.DMA((copies,)),
             pltpu.SemaphoreType.DMA((copies,)),

time: 42.3 us -> 37.3 us (0.88)
  Pallas kernels: 41.4 us -> 36.4 us
    pallas_call x1, Pallas kernels: 41.4 us -> 36.4 us  [on_device(): pl.pallas_call(kernel, out_shape=pltpu.VMEM((rows, cols, C), BF), in_spec...]
where the time goes in v5:
time: 37.3 us; the launch traced here: 37.2 us
  Pallas kernels  36.4 us (98%)
  local copies, waits for them, and re-layouts  0.8 us (2%)
    pallas_call x1, Pallas kernels, on_device(): pl.pallas_call(kernel, out_shape=pltpu.VMEM((rows, cols, C), BF), in_spec...  36.4 us
    unnamed x1, local copies, waits for them, and re-layouts  0.8 us

profile of v5, /device:TPU:1, one launch (start us, length us, event | category | flops | bytes accessed | tf_op | source)
XLA Modules:
  0.0 37.2 jit_solution(14856555283665426550)
XLA Ops:
  0.0 36.4 %swin_pair.1 = bf16[8,256,128]{2,1,0:T(8,128)(2,1)S(1)} custom-call(bf16[8,256,128]{2,1,0:T(8,128)(2,1)} %x_in.1, s32[8,256]{1,0:T(8,128)} %lab_in.1, s32[64,64]{1,0:T(8,128)} %rel_in.1, f32[2,2,128]{2,1,0:T(2,128)} %gain_in.1, f32[2,2,128]{2,1,0:T(2,128)} %shift_in.1, bf16[2,3,64,128]{3,2,1,0:T(8,128)(2,1)} %bitcast.3, f32[3,2,64]{2,1,0:T(2,128)} %bitcast.5, ...), custom_call_target="tpu_custom_call" | custom-call | tf_op jit(solution)/shard_map/swin_pair/pallas_call | solution.py:490
  36.4 0.8 %copy.16 = bf16[8,256,128]{2,1,0:T(8,128)(2,1)} copy(bf16[8,256,128]{2,1,0:T(8,128)(2,1)S(1)} %swin_pair.1) | data formatting | bytes 1048576

commit v6 on v5

--- a/solution.py
+++ b/solution.py
@@ -266,6 +266,25 @@
 
     lax.fori_loop(0, chunks, own_heads, 0)
 
+    def spread(line):
+        return jnp.broadcast_to(line.astype(F32), (128, 128)).T
+
+    def put_middle(row, middle):
+        for r in range(SHIFT):
+            for t in range(cols // 128):
+                ids[row + r, SHIFT + 128 * t : SHIFT + 128 * t + 128, :] = spread(
+                    middle[r : r + 1, 128 * t : 128 * t + 128]
+                )
+
+    def put_ends(row, before, after):
+        for r in range(SHIFT):
+            line = slice(r, r + 1)
+            ids[row + r, 0:SHIFT, :] = spread(before[line])[128 - SHIFT :]
+            ids[row + r, SHIFT + cols : 2 * SHIFT + cols, :] = spread(after[line])[0:SHIFT]
+
+    for half in range(2):
+        put_middle(SHIFT + SHIFT * half, region.at[half])
+
     for c in first:
         c.wait_recv()
     first_bias(1)
@@ -289,9 +308,6 @@
             total = total + dot(hidden, w2[side, b])
         return total.astype(BF).astype(F32)
 
-    for c in second:
-        c.wait_recv()
-
     def halo_copy(near, k):
         at = pl.ds(pl.multiple_of(k * CHUNK, CHUNK), CHUNK)
         to_down = towards(near)[0]
@@ -322,6 +338,12 @@
         at = pl.ds(pl.multiple_of(k * 64 * GROUP, 64 * GROUP), 64 * GROUP)
         q, key, v = project(normed[at, :], woth, 1)
         other = half_attention(1, q, key, v)
+
+        @pl.when(step == 0)
+        def _():
+            for c in second:
+                c.wait_recv()
+
         done = feed(0, att[at, :] + other, windows_of(base))
         for r in range(WIN):
             line = jnp.concatenate(
@@ -341,32 +363,15 @@
     lax.fori_loop(0, chunks, first_block, 0)
 
     pl.when(ch == 0)(lambda: pl.semaphore_wait(ready, len(strangers)))
-    for c in band_regions(False):
+    for c in band_regions(False) + corner_copies(False):
         c.start()
     for k in range(chunks):
         halo_copy(False, k).start()
-    for c in corner_copies(False):
-        c.start()
-
-    def spread(line):
-        return jnp.broadcast_to(line.astype(F32), (128, 128)).T
-
-    def put_ids(row, middle, before, after):
-        for r in range(SHIFT):
-            line = slice(r, r + 1)
-            for t in range(cols // 128):
-                ids[row + r, SHIFT + 128 * t : SHIFT + 128 * t + 128, :] = spread(
-                    middle[line, 128 * t : 128 * t + 128]
-                )
-            ids[row + r, 0:SHIFT, :] = spread(before[line])[128 - SHIFT :]
-            ids[row + r, SHIFT + cols : 2 * SHIFT + cols, :] = spread(after[line])[0:SHIFT]
 
     for c in side_regions:
         c.wait_recv()
     for half in range(2):
-        put_ids(
-            SHIFT + SHIFT * half, region.at[half], lab_side.at[0, half], lab_side.at[1, half]
-        )
+        put_ends(SHIFT + SHIFT * half, lab_side.at[0, half], lab_side.at[1, half])
 
     for c in third:
         c.wait_recv()
@@ -396,7 +401,8 @@
         for i in range(2):
             part = lab_corner.at[corner + i]
             copy(15 + corner + i, part, part, up).wait_recv()
-        put_ids(theirs, lab_row.at[above], lab_corner.at[corner + 1], lab_corner.at[corner])
+        put_middle(theirs, lab_row.at[above])
+        put_ends(theirs, lab_corner.at[corner + 1], lab_corner.at[corner])
         for i in range(2):
             part = corners.at[corner + i]
             copy(30 + corner + i, part, part, up).wait_recv()

time: 37.3 us -> 36.5 us (0.979)
  the two profiles are of different devices: /device:TPU:1 before, /device:TPU:99 now
where the time goes in v6:
time: 36.5 us; the launch traced here: 36.4 us
  Pallas kernels  35.6 us (98%)
  local copies, waits for them, and re-layouts  0.8 us (2%)
    pallas_call x1, Pallas kernels, on_device(): pl.pallas_call(kernel, out_shape=pltpu.VMEM((rows, cols, C), BF), in_spec...  35.6 us
    unnamed x1, local copies, waits for them, and re-layouts  0.8 us

profile of v6, /device:TPU:99, one launch (start us, length us, event | category | flops | bytes accessed | tf_op | source)
XLA Modules:
  0.0 36.4 jit_solution(17558944620715805283)
XLA Ops:
  0.0 35.6 %swin_pair.1 = bf16[8,256,128]{2,1,0:T(8,128)(2,1)S(1)} custom-call(bf16[8,256,128]{2,1,0:T(8,128)(2,1)} %x_in.1, s32[8,256]{1,0:T(8,128)} %lab_in.1, s32[64,64]{1,0:T(8,128)} %rel_in.1, f32[2,2,128]{2,1,0:T(2,128)} %gain_in.1, f32[2,2,128]{2,1,0:T(2,128)} %shift_in.1, bf16[2,3,64,128]{3,2,1,0:T(8,128)(2,1)} %bitcast.3, f32[3,2,64]{2,1,0:T(2,128)} %bitcast.5, ...), custom_call_target="tpu_custom_call" | custom-call | tf_op jit(solution)/shard_map/swin_pair/pallas_call | solution.py:496
  35.6 0.8 %copy.16 = bf16[8,256,128]{2,1,0:T(8,128)(2,1)} copy(bf16[8,256,128]{2,1,0:T(8,128)(2,1)S(1)} %swin_pair.1) | data formatting | bytes 1048576

commit v7 on v6

--- a/solution.py
+++ b/solution.py
@@ -49,7 +49,7 @@
     x, lab, rel, gain, shift, qkvb, tbl, wproj, projb, w1, b1, w2, fc2b,
     wown, woth, wfull, bqkv, bias0, bias1,
     y, ids, normed, att, region, lab_row, lab_side, lab_corner,
-    halo, both, sides, corners,
+    halo, both, patches, sides, corners,
     ready, local, send, recv,
 ):
     cols = x.shape[1]
@@ -316,20 +316,19 @@
             both.at[to_down, :, at], towards(near)[1][0],
         )
 
-    edge = {-1: pl.ds(0, 16), 1: pl.ds(cols - 16, 16)}
     side_copies = [
-        copy(28, halo.at[:, edge[-1]], sides.at[1], left),
-        copy(29, halo.at[:, edge[1]], sides.at[0], right),
+        copy(28, patches.at[0], sides.at[1], left),
+        copy(29, patches.at[1], sides.at[0], right),
     ]
 
     def corner_copies(near):
         to_down, (_, *diagonals) = towards(near)
         return [
             copy(
-                30 + 2 * to_down + i, halo.at[pl.ds(SHIFT * to_down, SHIFT), edge[side]],
+                30 + 2 * to_down + i, patches.at[i, to_down],
                 corners.at[2 * to_down + i], diagonals[i],
             )
-            for i, side in enumerate((-1, 1))
+            for i in range(2)
         ]
 
     def first_block(step, carry):
@@ -355,6 +354,12 @@
 
         @pl.when(step == 1)
         def _():
+            for e, at in enumerate((SHIFT, cols)):
+                for half in range(2):
+                    patches[e, half] = jnp.concatenate(
+                        [y[SHIFT + SHIFT * half + r, at : at + SHIFT, :] for r in range(SHIFT)],
+                        axis=0,
+                    ).astype(BF)
             for c in side_copies + corner_copies(True):
                 c.start()
 
@@ -377,10 +382,16 @@
         c.wait_recv()
     for c in side_copies:
         c.wait_recv()
-    ends = ((slice(0, SHIFT), slice(12, 16)), (slice(SHIFT + cols, 2 * SHIFT + cols), slice(0, SHIFT)))
-    for s, (to, of) in enumerate(ends):
-        for r in range(WIN):
-            y[SHIFT + r, to, :] = sides[s, r].astype(F32)[of]
+    ends = (slice(0, SHIFT), slice(SHIFT + cols, 2 * SHIFT + cols))
+
+    def put_patch(row, to, patch):
+        values = patch.astype(F32)
+        for r in range(SHIFT):
+            y[row + r, to, :] = values[SHIFT * r : SHIFT * r + SHIFT]
+
+    for s, to in enumerate(ends):
+        for half in range(2):
+            put_patch(SHIFT + SHIFT * half, to, sides[s, half])
 
     def shifted_band(is_bottom):
         mine = SHIFT + SHIFT * is_bottom
@@ -406,9 +417,7 @@
         for i in range(2):
             part = corners.at[corner + i]
             copy(30 + corner + i, part, part, up).wait_recv()
-            to, of = ends[1 - i]
-            for r in range(SHIFT):
-                y[theirs + r, to, :] = part[r].astype(F32)[of]
+            put_patch(theirs, ends[1 - i], part[...])
         take(0)
 
         def body(c, carry):
@@ -511,7 +520,7 @@
             V((2, SHIFT, cols), jnp.int32), V((2, SHIFT, cols), jnp.int32),
             V((2, 2, SHIFT, 128), jnp.int32), V((4, SHIFT, 128), jnp.int32),
             V((rows, cols, C), BF), V((2, SHIFT, cols, C), BF),
-            V((2, rows, 16, C), BF), V((4, SHIFT, 16, C), BF),
+            V((2, 2, 16, C), BF), V((2, 2, 16, C), BF), V((4, 16, C), BF),
             pltpu.SemaphoreType.REGULAR,
             pltpu.SemaphoreType.DMA((15,)),
             pltpu.SemaphoreType.DMA((copies,)),

time: 36.5 us -> 35.4 us (0.970)
  Pallas kernels: 35.6 us -> 34.5 us
    pallas_call x1, Pallas kernels: 35.6 us -> 34.5 us  [on_device(): pl.pallas_call(kernel, out_shape=pltpu.VMEM((rows, cols, C), BF), in_spec...]
where the time goes in v7:
time: 35.4 us; the launch traced here: 35.3 us
  Pallas kernels  34.5 us (97%)
  local copies, waits for them, and re-layouts  0.8 us (2%)
    pallas_call x1, Pallas kernels, on_device(): pl.pallas_call(kernel, out_shape=pltpu.VMEM((rows, cols, C), BF), in_spec...  34.5 us
    unnamed x1, local copies, waits for them, and re-layouts  0.8 us

profile of v7, /device:TPU:99, one launch (start us, length us, event | category | flops | bytes accessed | tf_op | source)
XLA Modules:
  0.0 35.3 jit_solution(7647054399621721443)
XLA Ops:
  0.0 34.5 %swin_pair.1 = bf16[8,256,128]{2,1,0:T(8,128)(2,1)S(1)} custom-call(bf16[8,256,128]{2,1,0:T(8,128)(2,1)} %x_in.1, s32[8,256]{1,0:T(8,128)} %lab_in.1, s32[64,64]{1,0:T(8,128)} %rel_in.1, f32[2,2,128]{2,1,0:T(2,128)} %gain_in.1, f32[2,2,128]{2,1,0:T(2,128)} %shift_in.1, bf16[2,3,64,128]{3,2,1,0:T(8,128)(2,1)} %bitcast.3, f32[3,2,64]{2,1,0:T(2,128)} %bitcast.5, ...), custom_call_target="tpu_custom_call" | custom-call | tf_op jit(solution)/shard_map/swin_pair/pallas_call | solution.py:505
  34.5 0.8 %copy.16 = bf16[8,256,128]{2,1,0:T(8,128)(2,1)} copy(bf16[8,256,128]{2,1,0:T(8,128)(2,1)S(1)} %swin_pair.1) | data formatting | bytes 1048576
